TPU v7x, 512 devices: a whole 4x4x16 slice. The times are simulated.
512 devices in a mesh: lon: 32 (over x_hi, z), lat: 16 (over x_lo, y, core).
Axes of the slice: x: 4 (x_hi: 2, x_lo: 2; x = x_hi * 2 + x_lo), y: 4, z: 16, core: 2. Of those that a mesh axis runs over, the one named last changes fastest.
Arguments:
- tracers: float32 [40, 8, 128, 4096], P(None, None, 'lat', 'lon'), may hold values from -6 to 6
- kmt: int32 [128, 4096], P('lat', 'lon'), may hold values from 0 to 8
Outputs:
- updated: float32 [40, 8, 128, 4096], P(None, None, 'lat', 'lon')
Inputs may be any that keep to these rules, and one draw needn't show every extreme that they name: Level k of column (j, i) is ocean exactly when k < kmt[j, i].
All inputs are finite; a program needn't handle non-finite values.
Results may differ from a plain program's by a relative error of at most 0.00002.
Values sent between devices are 32-bit elements; how exact they have to be, the bound alone decides.
A program may use at most 64 MiB of HBM per device.

v0:
```python
import jax
import jax.numpy as jnp
from jax import lax
from jax.sharding import PartitionSpec as P

THERMAL = 0.2
HALINE = 0.8
REDI_COEF = 0.1
SKEW_COEF = 0.05
SLOPE_MAX = 0.6
SLOPE_WIDTH = 0.2


def extended_2(shard, sides, width):
    edges = {}
    for axis, dim in sides:
        size, length = (lax.axis_size(axis), shard.shape[dim])
        up = [(i, (i + 1) % size) for i in range(size)]
        last = lax.slice_in_dim(shard, length - width, length, axis=dim)
        first = lax.slice_in_dim(shard, 0, width, axis=dim)
        edges[dim] = (
            lax.ppermute(last, axis, up),
            lax.ppermute(first, axis, [(b, a) for a, b in up]),
        )
    done = []
    for _, dim in sides:
        low, high = edges[dim]
        around = [(width, width) if d in done else (0, 0) for d in range(shard.ndim)]
        shard = jnp.concatenate([jnp.pad(low, around), shard, jnp.pad(high, around)], axis=dim)
        done.append(dim)
    return shard


def taper(slope):
    return slope * 0.5 * (1.0 + jnp.tanh((SLOPE_MAX - jnp.abs(slope)) / SLOPE_WIDTH))


def pad_levels(values):
    zero_layer = jnp.zeros_like(values[..., :1, :, :])
    return jnp.concatenate([zero_layer, values, zero_layer], axis=-3)


def slope_fields(density, wet_mask):
    level_mask = wet_mask[1:] * wet_mask[:-1]
    strat = (density[1:] - density[:-1]) * level_mask
    strat_pad = pad_levels(strat)
    strat_cell = 0.5 * (strat_pad[:-1] + strat_pad[1:])
    east_mask = wet_mask[:, 1:-1, :-1] * wet_mask[:, 1:-1, 1:]
    north_mask = wet_mask[:, :-1, 1:-1] * wet_mask[:, 1:, 1:-1]
    grad_east = (density[:, 1:-1, 1:] - density[:, 1:-1, :-1]) * east_mask
    strat_east = 0.5 * (strat_cell[:, 1:-1, 1:] + strat_cell[:, 1:-1, :-1])
    slope_x = taper(grad_east / jnp.maximum(strat_east, 1.0))
    grad_north = (density[:, 1:, 1:-1] - density[:, :-1, 1:-1]) * north_mask
    strat_north = 0.5 * (strat_cell[:, 1:, 1:-1] + strat_cell[:, :-1, 1:-1])
    slope_y = taper(grad_north / jnp.maximum(strat_north, 1.0))
    cell_x = 0.5 * (slope_x[..., :-1] + slope_x[..., 1:])
    cell_y = 0.5 * (slope_y[:, :-1, :] + slope_y[:, 1:, :])
    level_x = 0.5 * (cell_x[:-1] + cell_x[1:])
    level_y = 0.5 * (cell_y[:-1] + cell_y[1:])
    return (level_mask, east_mask, north_mask, slope_x, slope_y, level_x, level_y)


def tracer_step(field, fields):
    level_mask, east_mask, north_mask, slope_x, slope_y, level_x, level_y = fields
    vert_diff = (field[..., 1:, :, :] - field[..., :-1, :, :]) * level_mask
    vert_pad = pad_levels(vert_diff)
    vert_cell = 0.5 * (vert_pad[..., :-1, :, :] + vert_pad[..., 1:, :, :])
    grad_x = (field[..., 1:-1, 1:] - field[..., 1:-1, :-1]) * east_mask
    grad_y = (field[..., 1:, 1:-1] - field[..., :-1, 1:-1]) * north_mask
    flux_x = (
        -(
            REDI_COEF * grad_x
            + (REDI_COEF - SKEW_COEF)
            * slope_x
            * 0.5
            * (vert_cell[..., 1:-1, 1:] + vert_cell[..., 1:-1, :-1])
        )
        * east_mask
    )
    flux_y = (
        -(
            REDI_COEF * grad_y
            + (REDI_COEF - SKEW_COEF)
            * slope_y
            * 0.5
            * (vert_cell[..., 1:, 1:-1] + vert_cell[..., :-1, 1:-1])
        )
        * north_mask
    )
    cell_gx = 0.5 * (grad_x[..., :-1] + grad_x[..., 1:])
    cell_gy = 0.5 * (grad_y[..., :-1, :] + grad_y[..., 1:, :])
    level_gx = 0.5 * (cell_gx[..., :-1, :, :] + cell_gx[..., 1:, :, :])
    level_gy = 0.5 * (cell_gy[..., :-1, :, :] + cell_gy[..., 1:, :, :])
    flux_z = (
        -(
            (REDI_COEF + SKEW_COEF) * (level_x * level_gx + level_y * level_gy)
            + REDI_COEF * (level_x * level_x + level_y * level_y) * vert_diff[..., 1:-1, 1:-1]
        )
        * level_mask[:, 1:-1, 1:-1]
    )
    flux_pad = pad_levels(flux_z)
    tendency = -(
        flux_x[..., 1:]
        - flux_x[..., :-1]
        + (flux_y[..., 1:, :] - flux_y[..., :-1, :])
        + (flux_pad[..., 1:, :, :] - flux_pad[..., :-1, :, :])
    )
    return field[..., 1:-1, 1:-1] + tendency


def local(tracers, kmt):
    channels = tracers.shape[0]
    levels = tracers.shape[1]
    rows_here = tracers.shape[2]
    level_index = lax.broadcasted_iota(jnp.int32, (levels,) + kmt.shape, 0)
    wet_mask = (level_index < kmt[None]).astype(jnp.float32)
    stacked = jnp.concatenate([tracers, wet_mask[None]], axis=0)
    lat_index = lax.axis_index("lat")
    at_top = lat_index == lax.axis_size("lat") - 1
    extended = extended_2(stacked, (("lat", 2), ("lon", 3)), 1)
    south_row = jnp.where(lat_index == 0, 0.0, extended[:, :, 0, :])
    extended = extended.at[:, :, 0, :].set(south_row)
    edge_row = stacked[:, :, rows_here - 1, :]
    blocks = lax.axis_size("lon")
    columns = edge_row.shape[2]
    flat_rows = edge_row.shape[0] * edge_row.shape[1]
    padded_rows = -(-flat_rows // blocks) * blocks
    flat_edge = edge_row.reshape(flat_rows, columns)
    flat_edge = jnp.pad(flat_edge, ((0, padded_rows - flat_rows), (0, 0)))
    received = lax.all_to_all(flat_edge, "lon", split_axis=0, concat_axis=0, tiled=True)
    width = received.shape[1]
    slots = received.reshape(blocks, padded_rows // blocks, width)[::-1]
    returned = lax.all_to_all(
        slots.reshape(padded_rows, width), "lon", split_axis=0, concat_axis=0, tiled=True
    )
    partner = returned[:flat_rows].reshape(edge_row.shape)
    mirrored = partner[..., ::-1]
    north_row = jnp.where(at_top, mirrored, extended[:, :, rows_here + 1, 1:-1])
    extended = extended.at[:, :, rows_here + 1, 1:-1].set(north_row)
    density = HALINE * extended[1] - THERMAL * extended[0]
    fields = slope_fields(density, extended[channels])
    return tracer_step(extended[:channels], fields)


def solution(mesh):
    return jax.shard_map(
        local,
        mesh=mesh,
        in_specs=(P(None, None, "lat", "lon"), P("lat", "lon")),
        out_specs=P(None, None, "lat", "lon"),
        check_vma=False,
    )
```

profile of v0, /device:TPU:16, one launch (start us, length us, event | category | flops | bytes accessed | tf_op | source)
XLA Modules:
  0.0 90.4 jit_solution(2013679141725705480)
XLA Ops:
  0.0 1.6 %copy.15 = f32[40,8,8,128]{3,1,0,2:T(8,128)S(1)} copy(f32[40,8,8,128]{3,2,1,0:T(8,128)} %param.6) | data formatting | bytes 2621440 | tf_op args[0]
  1.7 0.9 all_to_all.14
  2.5 17.9 %all-to-all-start = ((f32[32,11,128]{2,1,0:T(8,128)}), f32[32,11,128]{2,1,0:T(8,128)S(1)}, u32[]{:S(2)}, u32[]{:S(2)}) async-start(f32[32,11,128]{2,1,0:T(8,128)} %all_to_all.14), calls=%async_computation | async-start | bytes 524288 | tf_op jit(solution)/shard_map/all_to_all | solution.py:130
  20.5 1.9 %collective-permute-start.1 = (f32[41,8,1,128]{3,1,0,2:T(8,128)S(1)}, f32[41,8,1,128]{3,1,0,2:T(8,128)S(1)}, u32[]{:S(2)}, u32[]{:S(2)}) collective-permute-start(f32[41,8,1,128]{3,1,0,2:T(8,128)S(1)} %get-tuple-element.43), channel_id=1, source_target_pairs={{0,1},{1,2},{2,3},{3,4},{4,5},{5,6},{6,7},{7,8},{8,9},{9,10},{10,1... | collective-permute-start | bytes 503816 | tf_op jit(solution)/shard_map/ppermute | solution.py:22
  22.4 3.6 %collective-permute-start.2 = (f32[41,8,1,128]{3,1,0,2:T(8,128)S(1)}, f32[41,8,1,128]{3,1,0,2:T(8,128)}, u32[]{:S(2)}, u32[]{:S(2)}) collective-permute-start(f32[41,8,1,128]{3,1,0,2:T(8,128)S(1)} %get-tuple-element.44), channel_id=1, source_target_pairs={{1,0},{2,1},{3,2},{4,3},{5,4},{6,5},{7,6},{8,7},{9,8},{10,9},{11,1... | collective-permute-start | bytes 503816 | tf_op jit(solution)/shard_map/ppermute | solution.py:23
  26.1 18.2 %all-to-all-done = f32[32,11,128]{2,1,0:T(8,128)S(1)} async-done(((f32[32,11,128]{2,1,0:T(8,128)}), f32[32,11,128]{2,1,0:T(8,128)S(1)}, u32[]{:S(2)}, u32[]{:S(2)}) %all-to-all-start) | async-done | bytes 180256 | tf_op jit(solution)/shard_map/all_to_all | solution.py:130
  44.2 0.7 all_to_all.16
  44.9 4.6 %all-to-all-start.1 = ((f32[32,11,128]{2,1,0:T(8,128)}), f32[32,11,128]{2,1,0:T(8,128)}, u32[]{:S(2)}, u32[]{:S(2)}) async-start(f32[32,11,128]{2,1,0:T(8,128)} %all_to_all.16), calls=%async_computation.1 | async-start | bytes 524288 | tf_op jit(solution)/shard_map/all_to_all | solution.py:133
  49.6 1.5 %fusion.11 = (f32[41,8,8,1]{3,1,0,2:T(8,128)}, f32[41,8,8,1]{3,1,0,2:T(8,128)S(1)}) fusion(f32[1,8,8,128]{3,1,0,2:T(8,128)S(1)} %fusion.44, f32[40,8,8,128]{3,1,0,2:T(8,128)S(1)} %copy.15), kind=kLoop, calls=%fused_computation.24 | loop fusion | flops 5248 | bytes 1364480 | tf_op jit(solution)/shard_map/concatenate | solution.py:117
  51.1 1.9 %copy.16 = f32[41,8,8,1]{0,2,3,1:T(8,128)S(1)} copy(f32[41,8,8,1]{3,1,0,2:T(8,128)} %get-tuple-element.45) | data formatting | bytes 20992 | tf_op jit(solution)/shard_map/slice | solution.py:19
  53.0 3.5 %collective-permute-start = (f32[41,8,8,1]{0,2,3,1:T(8,128)S(1)}, f32[41,8,8,1]{0,2,3,1:T(8,128)S(1)}, u32[]{:S(2)}, u32[]{:S(2)}) collective-permute-start(f32[41,8,8,1]{0,2,3,1:T(8,128)S(1)} %copy.16), channel_id=1, source_target_pairs={{0,16},{16,32},{32,48},{48,64},{64,80},{80,96},{96,112},{112,128},... | collective-permute-start | bytes 31496 | tf_op jit(solution)/shard_map/ppermute | solution.py:22
  56.5 0.7 copy.18
  57.1 6.1 %collective-permute-start.3 = (f32[41,8,8,1]{0,2,3,1:T(8,128)S(1)}, f32[41,8,8,1]{0,2,3,1:T(8,128)S(1)}, u32[]{:S(2)}, u32[]{:S(2)}) collective-permute-start(f32[41,8,8,1]{0,2,3,1:T(8,128)S(1)} %copy.18), channel_id=1, source_target_pairs={{16,0},{32,16},{48,32},{64,48},{80,64},{96,80},{112,96},{128,112},... | collective-permute-start | bytes 31496 | tf_op jit(solution)/shard_map/ppermute | solution.py:23
  63.3 0.7 collective-permute-done
  64.0 1.7 %copy.17 = f32[41,8,8,1]{3,1,0,2:T(8,128)} copy(f32[41,8,8,1]{0,2,3,1:T(8,128)S(1)} %collective-permute-done) | data formatting | bytes 20992 | tf_op jit(solution)/shard_map/ppermute | solution.py:22
  65.7 1.7 %copy.19 = f32[41,8,8,1]{3,1,0,2:T(8,128)} copy(f32[41,8,8,1]{0,2,3,1:T(8,128)S(1)} %collective-permute-done.3) | data formatting | bytes 20992 | tf_op jit(solution)/shard_map/ppermute | solution.py:23
  67.4 0.7 copy-done.1
  68.1 3.5 %select_maximum_fusion = f32[41,8,10,130]{3,1,0,2:T(8,128)S(1)} fusion(f32[41,8,8,1]{3,1,0,2:T(8,128)} %copy.19, f32[41,8,8,1]{3,1,0,2:T(8,128)} %copy.17, f32[41,8,1,128]{3,1,0,2:T(8,128)} %collective-permute-done.2, f32[1,8,8,128]{3,1,0,2:T(8,128)S(1)} %fusion.44, f32[40,8,8,128]{3,1,0,2:T(8,128)} %copy-done, f32[41,8,1,128]{3,1,0,2:T(8,128)} %copy-done.1), kind=kLoop, calls=%fused_computation | loop fusion | flops 3837600 | bytes 3405952 | tf_op jit(solution)/shard_map/concatenate | solution.py:29
  71.6 0.5 all-to-all-done.1
  72.1 1.0 %all_to_all.18 = f32[352,128]{1,0:T(8,128)S(1)} reshape(f32[32,11,128]{2,1,0:T(8,128)} %all-to-all-done.1) | data formatting | bytes 360448 | tf_op jit(solution)/shard_map/all_to_all | solution.py:133
  73.1 0.7 slice_bitcast_fusion.1
  73.8 1.7 %rev.4 = f32[41,8,128]{2,1,0:T(8,128)} reverse(f32[41,8,128]{2,1,0:T(8,128)} %slice_bitcast_fusion.1), dimensions={2} | reverse | bytes 335872 | tf_op jit(solution)/shard_map/rev | solution.py:137
  75.6 6.1 %scatter.9 = f32[41,8,10,130]{3,1,0,2:T(8,128)S(1)} dynamic-update-slice(f32[41,8,10,130]{3,1,0,2:T(8,128)S(1)} %fusion.25, f32[41,8,1,128]{3,1,0,2:T(8,128)S(1)} %fusion.29, s32[]{:T(128)} %constant.97.clone.1, s32[]{:T(128)} %constant.97.clone.1, s32[]{:T(128)} %constant.99.clone.1, s32[]{:T(128)} %constant.100.clone.1) | dynamic-update-slice | bytes 335876 | tf_op jit(solution)/shard_map/scatter | solution.py:139
  81.9 0.1 broadcast_multiply_fusion.1
  82.1 0.4 fusion
  82.6 0.6 add_multiply_fusion
  83.4 1.5 %fusion.4 = (f32[40,8,8,129]{3,1,0,2:T(8,128)S(1)}, f32[40,8,8,129]{3,1,0,2:T(8,128)S(1)}) fusion(f32[40,8,10,130]{3,1,0,2:T(8,128)S(1)} %add_multiply_fusion, f32[8,8,129]{2,0,1:T(8,128)S(1)} %get-tuple-element.31, f32[8,8,129]{2,0,1:T(8,128)S(1)} %get-tuple-element.33, f32[41,8,10,130]{3,1,0,2:T(8,128)S(1)} %scatter.9), kind=kLoop, calls=%fused_computation.11 | loop fusion | flops 2641920 | bytes 7991808 | tf_op jit(solution)/shard_map/mul | solution.py:71
  84.9 1.6 %fusion.9 = (f32[40,8,9,128]{3,1,0,2:T(8,128)S(1)}, f32[40,8,9,128]{3,1,0,2:T(8,128)S(1)}) fusion(f32[40,8,10,130]{3,1,0,2:T(8,128)S(1)} %add_multiply_fusion, f32[8,9,128]{2,0,1:T(8,128)S(1)} %get-tuple-element.36, f32[8,9,128]{2,0,1:T(8,128)S(1)} %get-tuple-element.38, f32[41,8,10,130]{3,1,0,2:T(8,128)S(1)} %scatter.9), kind=kLoop, calls=%fused_computation.21 | loop fusion | flops 2949120 | bytes 8921088 | tf_op jit(solution)/shard_map/mul | solution.py:81
  86.5 0.5 fusion.18
  86.9 0.8 fusion.14
  87.7 0.9 fusion.24
  88.6 1.8 %copy.21 = f32[40,8,8,128]{3,2,1,0:T(8,128)} copy(f32[40,8,8,128]{3,1,0,2:T(8,128)S(1)} %fusion.24) | data formatting | bytes 2621440 | tf_op jit(solution)/shard_map/add | solution.py:108
  (20 shorter events, 0.6 us)
Async XLA Ops:
  0.0 1.6 %copy-start.2 = (s32[8,128]{1,0:T(8,128)S(1)}, s32[8,128]{1,0:T(8,128)}, u32[]{:S(2)}) copy-start(s32[8,128]{1,0:T(8,128)} %param.7) | copy-start | bytes 12292
  1.6 47.9 %copy-start = (f32[40,8,8,128]{3,1,0,2:T(8,128)}, f32[40,8,8,128]{3,1,0,2:T(8,128)S(1)}, u32[]{:S(2)}) copy-start(f32[40,8,8,128]{3,1,0,2:T(8,128)S(1)} %copy.15) | copy-start | bytes 3932164
  2.5 41.7 %all-to-all-start = ((f32[32,11,128]{2,1,0:T(8,128)}), f32[32,11,128]{2,1,0:T(8,128)S(1)}, u32[]{:S(2)}, u32[]{:S(2)}) async-start(f32[32,11,128]{2,1,0:T(8,128)} %all_to_all.14), calls=%async_computation | async-start | bytes 524288 | tf_op jit(solution)/shard_map/all_to_all | solution.py:130
  20.5 46.9 %collective-permute-start.1 = (f32[41,8,1,128]{3,1,0,2:T(8,128)S(1)}, f32[41,8,1,128]{3,1,0,2:T(8,128)S(1)}, u32[]{:S(2)}, u32[]{:S(2)}) collective-permute-start(f32[41,8,1,128]{3,1,0,2:T(8,128)S(1)} %get-tuple-element.43), channel_id=1, source_target_pairs={{0,1},{1,2},{2,3},{3,4},{4,5},{5,6},{6,7},{7,8},{8,9},{9,10},{10,1... | collective-permute-start | bytes 503816 | tf_op jit(solution)/shard_map/ppermute | solution.py:22
  22.4 45.7 %collective-permute-start.2 = (f32[41,8,1,128]{3,1,0,2:T(8,128)S(1)}, f32[41,8,1,128]{3,1,0,2:T(8,128)}, u32[]{:S(2)}, u32[]{:S(2)}) collective-permute-start(f32[41,8,1,128]{3,1,0,2:T(8,128)S(1)} %get-tuple-element.44), channel_id=1, source_target_pairs={{1,0},{2,1},{3,2},{4,3},{5,4},{6,5},{7,6},{8,7},{9,8},{10,9},{11,1... | collective-permute-start | bytes 503816 | tf_op jit(solution)/shard_map/ppermute | solution.py:23
  44.9 27.2 %all-to-all-start.1 = ((f32[32,11,128]{2,1,0:T(8,128)}), f32[32,11,128]{2,1,0:T(8,128)}, u32[]{:S(2)}, u32[]{:S(2)}) async-start(f32[32,11,128]{2,1,0:T(8,128)} %all_to_all.16), calls=%async_computation.1 | async-start | bytes 524288 | tf_op jit(solution)/shard_map/all_to_all | solution.py:133
  53.0 11.0 %collective-permute-start = (f32[41,8,8,1]{0,2,3,1:T(8,128)S(1)}, f32[41,8,8,1]{0,2,3,1:T(8,128)S(1)}, u32[]{:S(2)}, u32[]{:S(2)}) collective-permute-start(f32[41,8,8,1]{0,2,3,1:T(8,128)S(1)} %copy.16), channel_id=1, source_target_pairs={{0,16},{16,32},{32,48},{48,64},{64,80},{80,96},{96,112},{112,128},... | collective-permute-start | bytes 31496 | tf_op jit(solution)/shard_map/ppermute | solution.py:22
  57.1 8.5 %collective-permute-start.3 = (f32[41,8,8,1]{0,2,3,1:T(8,128)S(1)}, f32[41,8,8,1]{0,2,3,1:T(8,128)S(1)}, u32[]{:S(2)}, u32[]{:S(2)}) collective-permute-start(f32[41,8,8,1]{0,2,3,1:T(8,128)S(1)} %copy.18), channel_id=1, source_target_pairs={{16,0},{32,16},{48,32},{64,48},{80,64},{96,80},{112,96},{128,112},... | collective-permute-start | bytes 31496 | tf_op jit(solution)/shard_map/ppermute | solution.py:23
  67.4 0.7 copy-start.1
where the time goes:
time: 90.9 us; the launch traced here: 90.4 us
  starting transfers between devices  37.7 us (41%)
  local copies, waits for them, and re-layouts  21.2 us (23%)
  waiting for transfers between devices  19.4 us (21%)
  other arithmetic  11.8 us (13%)
    all_to_all x1, waiting for transfers between devices, local(): lax.all_to_all(flat_edge, 'lon', split_axis=0, concat_axis=0, tiled=True)  18.2 us
    all_to_all x1, starting transfers between devices, local(): lax.all_to_all(flat_edge, 'lon', split_axis=0, concat_axis=0, tiled=True)  17.9 us
    ppermute x2, starting transfers between devices, extended_2(): lax.ppermute(first, axis, [(b, a) for a, b in up])  9.77 us
    scatter x1, local copies, waits for them, and re-layouts, local(): extended = extended.at[:, :, rows_here + 1, 1:-1].set(north_row)  6.14 us
    ppermute x2, starting transfers between devices, extended_2(): lax.ppermute(last, axis, up)  5.42 us
    all_to_all x1, starting transfers between devices, local(): lax.all_to_all(slots.reshape(padded_rows, width), 'lon', split_axis=0, co...  4.58 us
    concatenate x1, other arithmetic, extended_2(): jnp.concatenate([jnp.pad(low, around), shard, jnp.pad(high, around)], axi...  3.45 us
    unnamed x7, local copies, waits for them, and re-layouts  2.27 us
  transfers between devices with their start and end apart: 6, of which 3 were waited for; matrix products, arithmetic and copies ran while one was open for 12% of the time, Pallas kernels for 0%

commit v1 on v0

v1 whole, which is shorter than its diff:
```python
import functools

import jax
import jax.numpy as jnp
from jax import lax
from jax.experimental import pallas as pl
from jax.experimental.pallas import tpu as pltpu
from jax.sharding import PartitionSpec as P

THERMAL = 0.2
HALINE = 0.8
REDI_COEF = 0.1
SKEW_COEF = 0.05
SLOPE_MAX = 0.6
SLOPE_WIDTH = 0.2
SLOPE_FLUX = (REDI_COEF - SKEW_COEF) * 0.25
CROSS = (REDI_COEF + SKEW_COEF) * 0.25 / REDI_COEF

ROWS = 8
LANES = 128
LEVELS = 8
MESH = pl.DeviceIdType.MESH
VMEM = pltpu.VMEM


def taper(slope):
    return slope * 0.5 * (1.0 + jnp.tanh((SLOPE_MAX - jnp.abs(slope)) / SLOPE_WIDTH))


def slope_of(step, mask, strat_twice):
    return taper(step * mask / jnp.maximum(0.25 * strat_twice, 1.0))


def below(limit, level):
    return jnp.where(level < limit, 1.0, 0.0)


def vertical_pair(values, mask, axis):
    size = values.shape[axis]
    diff = (pltpu.roll(values, size - 1, axis) - values) * mask
    return diff, diff + pltpu.roll(diff, 1, axis)


def up_one(values, axis):
    return pltpu.roll(values, values.shape[axis] - 1, axis)


def kernel(
    channels, chunks, tracers, kmt, out,
    field, row_south, row_inner, row_north, depth,
    from_south, from_north, depth_south, depth_north,
    to_west, to_east, from_west, from_east,
    coef, edge_x, row_coef,
    load_sem, send_sem, recv_sem,
):
    lon, lat = lax.axis_index("lon"), lax.axis_index("lat")
    blocks, bands = lax.axis_size("lon"), lax.axis_size("lat")
    top, bottom = lat == bands - 1, lat == 0
    west = (lax.rem(lon + blocks - 1, blocks), lat)
    east = (lax.rem(lon + 1, blocks), lat)
    north = (jnp.where(top, blocks - 1 - lon, lon), jnp.where(top, lat, lat + 1))
    south = (lon, jnp.maximum(lat - 1, 0))
    groups = to_west.shape[0]
    per_chunk = channels // chunks

    barrier = pltpu.get_barrier_semaphore()
    for other in (north, west, east):
        pl.semaphore_signal(barrier, inc=1, device_id=other, device_id_type=MESH)

    @pl.when(jnp.logical_not(bottom))
    def _():
        pl.semaphore_signal(barrier, inc=1, device_id=south, device_id_type=MESH)

    loads = [
        pltpu.make_async_copy(tracers.at[:, :, ROWS - 1, :], row_north, load_sem.at[0]),
        pltpu.make_async_copy(tracers, field, load_sem.at[1]),
        pltpu.make_async_copy(kmt, depth, load_sem.at[2]),
        pltpu.make_async_copy(tracers.at[:, :, 0, :], row_south, load_sem.at[3]),
        pltpu.make_async_copy(tracers.at[:, :, ROWS - 2, :], row_inner, load_sem.at[4]),
    ]
    for load in loads:
        load.start()
    for load in loads:
        load.wait()

    shape = (ROWS, LANES)
    lane = lax.broadcasted_iota(jnp.int32, shape, 1)
    row = lax.broadcasted_iota(jnp.int32, shape, 0)
    per_group = LANES // LEVELS
    depth_here = depth[...]
    depth_real = depth_here.astype(jnp.float32)

    for side, packed in ((0, to_west), (LANES - 1, to_east)):
        for group in range(groups):
            count = min(per_group, channels - group * per_group)

            def place(slot, total, group=group, side=side):
                piece = jnp.zeros(shape, jnp.float32)
                for level in range(LEVELS):
                    column = field[group * per_group + slot, level]
                    column = pltpu.roll(column, (level - side) % LANES, 1)
                    piece = jnp.where(lane == level, column, piece)
                piece = pltpu.roll(piece, slot * LEVELS, 1)
                return jnp.where(lane // LEVELS == slot, piece, total)

            total = lax.fori_loop(0, count, place, jnp.zeros(shape, jnp.float32))
            if group == groups - 1:
                at = count * LEVELS
                total = jnp.where(lane == at, pltpu.roll(depth_real, (at - side) % LANES, 1), total)
            packed[group] = total

    pl.semaphore_wait(barrier, jnp.where(bottom, 3, 4))

    def send(source, target, slot, device, send_slot=None):
        return pltpu.make_async_remote_copy(
            src_ref=source,
            dst_ref=target,
            send_sem=send_sem.at[slot if send_slot is None else send_slot],
            recv_sem=recv_sem.at[slot],
            device_id=device,
            device_id_type=MESH,
        )

    def to_north_halo(source, depth_row, device, first_send):
        copies = [send(depth_row, depth_north, 0, device, first_send)]
        for chunk in range(chunks):
            part = pl.ds(chunk * per_chunk, per_chunk)
            slot = 1 + chunk
            copies.append(send(source.at[part], from_north.at[part], slot, device, first_send + slot))
        return copies

    base = 1 + chunks
    own_south = depth.at[pl.ds(0, 1)]
    own_north = depth.at[pl.ds(ROWS - 1, 1)]
    fold = to_north_halo(row_north, own_north, north, base + 4)
    down = to_north_halo(row_south, own_south, south, 0)
    upward = [
        send(own_north, depth_south, base, north),
        send(row_north, from_south, base + 1, north),
    ]
    across = [
        send(to_west, from_east, base + 2, west),
        send(to_east, from_west, base + 3, east),
    ]

    @pl.when(top)
    def _():
        for copy in fold:
            copy.start()

    for copy in across:
        copy.start()

    @pl.when(jnp.logical_not(top))
    def _():
        for copy in upward:
            copy.start()

    @pl.when(jnp.logical_not(bottom))
    def _():
        for copy in down:
            copy.start()

    @pl.when(bottom)
    def _():
        from_south[...] = jnp.zeros_like(from_south)
        depth_south[...] = jnp.zeros_like(depth_south)

    for copy in across:
        copy.wait_recv()

    @pl.when(jnp.logical_not(bottom))
    def _():
        for copy in upward:
            copy.wait_recv()

    spot = groups - 1
    spot_lane = (channels * LEVELS) % LANES
    part_level = lane % LEVELS

    def side_column(packed):
        first = packed[0]
        density = HALINE * pltpu.roll(first, LANES - LEVELS, 1) - THERMAL * first
        limit = packed[spot][:, spot_lane : spot_lane + 1]
        limit = jnp.broadcast_to(limit, shape).astype(jnp.int32)
        _, strat = vertical_pair(density, below(limit, part_level + 1), 1)
        return density, strat, limit

    west_density, west_strat, west_limit = side_column(from_west)
    east_density, east_strat, east_limit = side_column(from_east)

    south_density = HALINE * from_south[1] - THERMAL * from_south[0]
    south_limit = depth_south[...]
    row_level = row
    south_mask = below(jnp.broadcast_to(south_limit, shape), row_level + 1)
    _, south_strat = vertical_pair(south_density, south_mask, 0)

    density = [HALINE * field[1, k] - THERMAL * field[0, k] for k in range(LEVELS)]
    level_mask = [below(depth_here, k + 1) for k in range(LEVELS - 1)]
    strat_face = [(density[k + 1] - density[k]) * level_mask[k] for k in range(LEVELS - 1)]
    strat = [strat_face[0]]
    strat += [strat_face[k - 1] + strat_face[k] for k in range(1, LEVELS - 1)]
    strat += [strat_face[LEVELS - 2]]
    depth_west = jnp.minimum(depth_here, jnp.where(lane == 0, west_limit, pltpu.roll(depth_here, 1, 1)))
    depth_east = jnp.minimum(
        depth_here, jnp.where(lane == LANES - 1, east_limit, pltpu.roll(depth_here, LANES - 1, 1))
    )
    depth_down = jnp.minimum(
        depth_here,
        jnp.where(row == 0, jnp.broadcast_to(south_limit, shape), pltpu.roll(depth_here, 1, 0)),
    )
    inner_x = jnp.where(lane > 0, 1.0, 0.0)
    inner_y = jnp.where(row > 0, 1.0, 0.0)
    lower_rows = jnp.where(row < ROWS - 1, 1.0, 0.0)
    sum_x, sum_y, faces = [], [], []
    for k in range(LEVELS):
        mask_w, mask_e, mask_s = (below(limit, k) for limit in (depth_west, depth_east, depth_down))

        def from_side(edge, values, packed, shift):
            return jnp.where(lane == edge, pltpu.roll(packed, (edge - k) % LANES, 1), pltpu.roll(values, shift, 1))

        def from_below(values, compact):
            edge = jnp.broadcast_to(compact[k : k + 1], shape)
            return jnp.where(row == 0, edge, pltpu.roll(values, 1, 0))

        slope_w = slope_of(
            density[k] - from_side(0, density[k], west_density, 1),
            mask_w,
            strat[k] + from_side(0, strat[k], west_strat, 1),
        )
        slope_e = slope_of(
            from_side(LANES - 1, density[k], east_density, LANES - 1) - density[k],
            mask_e,
            strat[k] + from_side(LANES - 1, strat[k], east_strat, LANES - 1),
        )
        slope_s = slope_of(
            density[k] - from_below(density[k], south_density),
            mask_s,
            strat[k] + from_below(strat[k], south_strat),
        )
        slope_n = up_one(slope_s, 0) * lower_rows
        sum_x.append(slope_w + slope_e)
        sum_y.append(slope_s + slope_n)
        faces.append((mask_w, mask_e, mask_s, slope_w, slope_e, slope_s))

    zero = jnp.zeros(shape, jnp.float32)
    edges = [zero] * 6
    for k in range(LEVELS):
        mask_w, mask_e, mask_s, slope_w, slope_e, slope_s = faces[k]
        grad_w, flux_w = REDI_COEF * mask_w, SLOPE_FLUX * slope_w
        grad_e, flux_e = REDI_COEF * mask_e, SLOPE_FLUX * slope_e
        grad_s, flux_s = REDI_COEF * mask_s, SLOPE_FLUX * slope_s
        coef[0, k] = grad_w * inner_x
        coef[1, k] = flux_w * inner_x
        coef[2, k] = grad_s * inner_y
        coef[3, k] = flux_s * inner_y
        row_coef[0, pl.ds(k, 1)] = grad_s[0:1]
        row_coef[1, pl.ds(k, 1)] = flux_s[0:1]
        row_coef[3, pl.ds(k, 1)] = grad_s[ROWS - 1 : ROWS]
        row_coef[4, pl.ds(k, 1)] = slope_s[ROWS - 1 : ROWS]
        if k < LEVELS - 1:
            mean_x = 0.25 * (sum_x[k] + sum_x[k + 1])
            mean_y = 0.25 * (sum_y[k] + sum_y[k + 1])
            cross_x = CROSS * mean_x * level_mask[k]
            cross_y = CROSS * mean_y * level_mask[k]
            square = REDI_COEF * (mean_x * mean_x + mean_y * mean_y)
            coef[7, k] = level_mask[k]
        else:
            mean_x, cross_x, cross_y, square = zero, zero, zero, zero
            coef[7, k] = zero
        coef[4, k] = cross_x
        coef[5, k] = cross_y * lower_rows
        coef[6, k] = square * lower_rows
        row_coef[2, pl.ds(k, 1)] = cross_y[0:1]
        row_coef[5, pl.ds(k, 1)] = mean_x[ROWS - 1 : ROWS]
        news = (
            (grad_w, 0), (flux_w, 0), (cross_x, 0),
            (grad_e, LANES - 1), (flux_e, LANES - 1), (cross_x, LANES - 1),
        )
        edges = [
            jnp.where(part_level == k, jnp.broadcast_to(new[:, at : at + 1], shape), old)
            for (new, at), old in zip(news, edges)
        ]

    here_w = below(jnp.broadcast_to(depth_here[:, 0:1], shape), part_level + 1)
    here_e = below(jnp.broadcast_to(depth_here[:, LANES - 1 : LANES], shape), part_level + 1)
    there_w, there_e = below(west_limit, part_level + 1), below(east_limit, part_level + 1)
    for group in range(groups):
        own, other = to_west[group], from_west[group]
        grad = edges[0] * (own - other)
        pair = vertical_pair(own, here_w, 1)[1] + vertical_pair(other, there_w, 1)[1]
        vertical = edges[2] * (grad + up_one(grad, 1))
        edge_x[0, group] = vertical - pltpu.roll(vertical, 1, 1) - (grad + edges[1] * pair)
        own, other = to_east[group], from_east[group]
        grad = edges[3] * (other - own)
        pair = vertical_pair(own, here_e, 1)[1] + vertical_pair(other, there_e, 1)[1]
        vertical = edges[5] * (grad + up_one(grad, 1))
        edge_x[1, group] = vertical - pltpu.roll(vertical, 1, 1) + (grad + edges[4] * pair)

    own_south_limit = jnp.broadcast_to(depth_here[0:1], shape)
    own_south_mask = below(own_south_limit, row_level + 1)
    own_north_limit = jnp.broadcast_to(depth_here[ROWS - 1 : ROWS], shape)
    own_north_mask = below(own_north_limit, row_level + 1)

    def one_tracer(tracer, carry):
        values = [field[tracer, k] for k in range(LEVELS)]
        diff = [(values[k + 1] - values[k]) * coef[7, k] for k in range(LEVELS - 1)]
        pair = [diff[0]] + [diff[k - 1] + diff[k] for k in range(1, LEVELS - 1)] + [diff[LEVELS - 2]]
        group, slot = tracer // per_group, lax.rem(tracer, per_group)
        edge_w = pltpu.roll(edge_x[0, group], LANES - slot * LEVELS, 1)
        edge_e = pltpu.roll(edge_x[1, group], LANES - slot * LEVELS, 1)
        grads_x, grads_y, sides = [], [], []
        for k in range(LEVELS):
            grad_w = coef[0, k] * (values[k] - pltpu.roll(values[k], 1, 1))
            flux_w = grad_w + coef[1, k] * (pair[k] + pltpu.roll(pair[k], 1, 1))
            grad_s = coef[2, k] * (values[k] - pltpu.roll(values[k], 1, 0))
            flux_s = grad_s + coef[3, k] * (pair[k] + pltpu.roll(pair[k], 1, 0))
            grads_x.append(grad_w + up_one(grad_w, 1))
            grads_y.append(grad_s + up_one(grad_s, 0))
            side = jnp.where(lane == LANES - 1, pltpu.roll(edge_e, LANES - 1 - k, 1), zero)
            side = jnp.where(lane == 0, pltpu.roll(edge_w, (LANES - k) % LANES, 1), side)
            sides.append(values[k] + (up_one(flux_w, 1) - flux_w) + (up_one(flux_s, 0) - flux_s) + side)
        above = None
        for k in range(LEVELS):
            total = sides[k]
            if k < LEVELS - 1:
                vertical = (
                    coef[4, k] * (grads_x[k] + grads_x[k + 1])
                    + coef[5, k] * (grads_y[k] + grads_y[k + 1])
                    + coef[6, k] * diff[k]
                )
                total = total + vertical
            else:
                vertical = None
            if above is not None:
                total = total - above
            out[tracer, k] = total
            above = vertical
        own, other = row_south[tracer], from_south[tracer]
        grad = row_coef[0] * (own - other)
        both = vertical_pair(own, own_south_mask, 0)[1] + vertical_pair(other, south_mask, 0)[1]
        vertical = row_coef[2] * (grad + up_one(grad, 0))
        change = vertical - pltpu.roll(vertical, 1, 0) - (grad + row_coef[1] * both)
        out[tracer, :, 0, :] = out[tracer, :, 0, :] + change
        return carry

    lax.fori_loop(0, channels, one_tracer, 0)

    source_lane = jnp.where(top, LANES - 1 - lane, lane)

    def arranged(values):
        return jnp.take_along_axis(values, source_lane, axis=1, mode="promise_in_bounds")

    down[0].wait_recv()
    down[1].wait_recv()
    north_limit = arranged(jnp.broadcast_to(depth_north[...], shape))
    north_mask = below(north_limit, row_level + 1)
    face_mask = below(jnp.minimum(own_north_limit, north_limit), row_level)
    own_density = HALINE * row_north[1] - THERMAL * row_north[0]
    north_density = arranged(HALINE * from_north[1] - THERMAL * from_north[0])
    _, own_strat = vertical_pair(own_density, own_north_mask, 0)
    _, north_strat = vertical_pair(north_density, north_mask, 0)
    slope_n = slope_of(north_density - own_density, face_mask, own_strat + north_strat)
    sum_n = slope_n + row_coef[4]
    mean_n = 0.25 * (sum_n + up_one(sum_n, 0))
    mean_x = row_coef[5]
    cross_n = CROSS * mean_n * own_north_mask
    square_n = REDI_COEF * (mean_x * mean_x + mean_n * mean_n)
    grad_n, flux_n, grad_in = REDI_COEF * face_mask, SLOPE_FLUX * slope_n, row_coef[3]

    def north_face(tracer, carry):
        own, other = row_north[tracer], arranged(from_north[tracer])
        grad = grad_n * (other - own)
        diff, pair = vertical_pair(own, own_north_mask, 0)
        both = pair + vertical_pair(other, north_mask, 0)[1]
        grads = grad + grad_in * (own - row_inner[tracer])
        vertical = cross_n * (grads + up_one(grads, 0)) + square_n * diff
        change = vertical - pltpu.roll(vertical, 1, 0) + (grad + flux_n * both)
        out[tracer, :, ROWS - 1, :] = out[tracer, :, ROWS - 1, :] + change
        return carry

    for chunk in range(chunks):
        if chunk:
            down[1 + chunk].wait_recv()
        lax.fori_loop(chunk * per_chunk, (chunk + 1) * per_chunk, north_face, 0)

    for copy in across:
        copy.wait_send()

    @pl.when(top)
    def _():
        for copy in fold:
            copy.wait_send()

    @pl.when(jnp.logical_not(top))
    def _():
        for copy in upward:
            copy.wait_send()

    @pl.when(jnp.logical_not(bottom))
    def _():
        for copy in down:
            copy.wait_send()


def local(tracers, kmt):
    channels = tracers.shape[0]
    chunks = 4
    groups = -(-(channels * LEVELS + 1) // LANES)
    row_array = VMEM((channels, LEVELS, LANES), jnp.float32)
    packed = VMEM((groups, ROWS, LANES), jnp.float32)
    depth_row = VMEM((1, LANES), jnp.int32)
    anywhere = pl.BlockSpec(memory_space=pl.ANY)
    return pl.pallas_call(
        functools.partial(kernel, channels, chunks),
        out_shape=jax.ShapeDtypeStruct(tracers.shape, jnp.float32),
        in_specs=[anywhere, anywhere],
        out_specs=pl.BlockSpec(memory_space=VMEM),
        scratch_shapes=[
            VMEM(tracers.shape, jnp.float32),
            row_array, row_array, row_array, VMEM((ROWS, LANES), jnp.int32),
            row_array, row_array, depth_row, depth_row,
            packed, packed, packed, packed,
            VMEM((8, LEVELS, ROWS, LANES), jnp.float32),
            VMEM((2, groups, ROWS, LANES), jnp.float32),
            VMEM((6, LEVELS, LANES), jnp.float32),
            pltpu.SemaphoreType.DMA((5,)),
            pltpu.SemaphoreType.DMA((2 * chunks + 6,)),
            pltpu.SemaphoreType.DMA((chunks + 5,)),
        ],
        compiler_params=pltpu.CompilerParams(collective_id=0, has_side_effects=True),
        name="tracer_step",
    )(tracers, kmt)


def solution(mesh):
    return jax.shard_map(
        local,
        mesh=mesh,
        in_specs=(P(None, None, "lat", "lon"), P("lat", "lon")),
        out_specs=P(None, None, "lat", "lon"),
        check_vma=False,
    )
```

time: 90.9 us -> 48.8 us (0.54)
  the two profiles are of different devices: /device:TPU:16 before, /device:TPU:27 now
where the time goes in v1:
time: 48.8 us; the launch traced here: 48.7 us
  Pallas kernels  46.1 us (94%)
  local copies, waits for them, and re-layouts  2.52 us (5%)
    pallas_call x1, Pallas kernels, local(): pl.pallas_call(functools.partial(kernel, channels, chunks), out_shape=jax...  46.1 us
    unnamed x1, local copies, waits for them, and re-layouts  2.52 us

profile of v1, /device:TPU:27, one launch (start us, length us, event | category | flops | bytes accessed | tf_op | source)
XLA Modules:
  0.0 48.7 jit_solution(18272169292938253989)
XLA Ops:
  0.0 46.1 %tracer_step.1 = f32[40,8,8,128]{3,2,1,0:T(8,128)} custom-call(f32[40,8,8,128]{3,2,1,0:T(8,128)} %tracers.1, s32[8,128]{1,0:T(8,128)} %kmt.1), custom_call_target="tpu_custom_call" | custom-call | tf_op jit(solution)/shard_map/tracer_step/pallas_call | solution.py:414
  46.1 2.5 %copy.4 = f32[40,8,8,128]{3,2,1,0:T(8,128)} copy(f32[40,8,8,128]{3,2,1,0:T(8,128)} %tracer_step.1) | data formatting | bytes 2621440

commit v2 on v1

v2 whole, which is shorter than its diff:
```python
import functools

import jax
import jax.numpy as jnp
from jax import lax
from jax.experimental import pallas as pl
from jax.experimental.pallas import tpu as pltpu
from jax.sharding import PartitionSpec as P

THERMAL = 0.2
HALINE = 0.8
REDI_COEF = 0.1
SKEW_COEF = 0.05
SLOPE_MAX = 0.6
SLOPE_WIDTH = 0.2
SLOPE_FLUX = (REDI_COEF - SKEW_COEF) * 0.25
CROSS = (REDI_COEF + SKEW_COEF) * 0.25 / REDI_COEF

ROWS = 8
LANES = 128
LEVELS = 8
MESH = pl.DeviceIdType.MESH
VMEM = pltpu.VMEM


def taper(slope):
    return slope * 0.5 * (1.0 + jnp.tanh((SLOPE_MAX - jnp.abs(slope)) / SLOPE_WIDTH))


def slope_of(step, mask, strat_twice):
    return taper(step * mask / jnp.maximum(0.25 * strat_twice, 1.0))


def below(limit, level):
    return jnp.where(level < limit, 1.0, 0.0)


def vertical_pair(values, mask, axis):
    size = values.shape[axis]
    diff = (pltpu.roll(values, size - 1, axis) - values) * mask
    return diff, diff + pltpu.roll(diff, 1, axis)


def up_one(values, axis):
    return pltpu.roll(values, values.shape[axis] - 1, axis)


def kernel(
    channels, chunks, tracers, kmt, out,
    field, row_south, row_inner, row_north, depth,
    from_south, from_north, depth_south, depth_north,
    sides, from_west, from_east,
    coef, part, edge, row_coef,
    load_sem, send_sem, recv_sem,
):
    lon, lat = lax.axis_index("lon"), lax.axis_index("lat")
    blocks, bands = lax.axis_size("lon"), lax.axis_size("lat")
    top, bottom = lat == bands - 1, lat == 0
    west = (lax.rem(lon + blocks - 1, blocks), lat)
    east = (lax.rem(lon + 1, blocks), lat)
    north = (jnp.where(top, blocks - 1 - lon, lon), jnp.where(top, lat, lat + 1))
    south = (lon, jnp.maximum(lat - 1, 0))
    per_chunk = channels // chunks

    barrier = pltpu.get_barrier_semaphore()
    for other in (north, west, east):
        pl.semaphore_signal(barrier, inc=1, device_id=other, device_id_type=MESH)

    @pl.when(jnp.logical_not(bottom))
    def _():
        pl.semaphore_signal(barrier, inc=1, device_id=south, device_id_type=MESH)

    loads = [
        pltpu.make_async_copy(kmt, depth, load_sem.at[2]),
        pltpu.make_async_copy(tracers, field, load_sem.at[1]),
        pltpu.make_async_copy(tracers.at[:, :, ROWS - 1, :], row_north, load_sem.at[0]),
        pltpu.make_async_copy(tracers.at[:, :, 0, :], row_south, load_sem.at[3]),
        pltpu.make_async_copy(tracers.at[:, :, ROWS - 2, :], row_inner, load_sem.at[4]),
    ]
    for load in loads:
        load.start()
    for load in loads:
        load.wait()

    shape = (ROWS, LANES)
    lane = lax.broadcasted_iota(jnp.int32, shape, 1)
    row = lax.broadcasted_iota(jnp.int32, shape, 0)
    zero = jnp.zeros(shape, jnp.float32)
    depth_here = depth[...]

    def right(values, count=1):
        return pltpu.roll(values, count % LANES, 1)

    def wide(values):
        return jnp.broadcast_to(values, shape)

    density = [HALINE * field[1, k] - THERMAL * field[0, k] for k in range(LEVELS)]
    level_mask = [below(depth_here, k + 1) for k in range(LEVELS - 1)]
    strat_face = [(density[k + 1] - density[k]) * level_mask[k] for k in range(LEVELS - 1)]
    strat = [strat_face[0]]
    strat += [strat_face[k - 1] + strat_face[k] for k in range(1, LEVELS - 1)]
    strat += [strat_face[LEVELS - 2]]
    depth_left = jnp.minimum(depth_here, jnp.where(lane == 0, 0, right(depth_here)))
    depth_right = jnp.minimum(depth_here, jnp.where(lane == LANES - 1, 0, right(depth_here, -1)))
    depth_down = jnp.minimum(depth_here, jnp.where(row == 0, 0, pltpu.roll(depth_here, 1, 0)))
    for k in range(LEVELS):
        mask_w, mask_e, mask_s = (below(limit, k) for limit in (depth_left, depth_right, depth_down))
        slope_w = slope_of(density[k] - right(density[k]), mask_w, strat[k] + right(strat[k]))
        slope_e = slope_of(right(density[k], -1) - density[k], mask_e, strat[k] + right(strat[k], -1))
        slope_s = slope_of(
            density[k] - pltpu.roll(density[k], 1, 0), mask_s, strat[k] + pltpu.roll(strat[k], 1, 0)
        )
        coef[0, k] = REDI_COEF * mask_w
        coef[1, k] = REDI_COEF * mask_e
        coef[2, k] = REDI_COEF * mask_s
        coef[3, k] = SLOPE_FLUX * slope_w
        coef[4, k] = SLOPE_FLUX * slope_e
        coef[5, k] = SLOPE_FLUX * slope_s
        coef[6, k] = level_mask[k] if k < LEVELS - 1 else zero
        coef[7, k] = slope_w + slope_e
        coef[8, k] = slope_s + up_one(slope_s, 0)
        row_coef[0, pl.ds(k, 1)] = slope_s[ROWS - 1 : ROWS]
        row_coef[1, pl.ds(k, 1)] = mask_s[ROWS - 1 : ROWS]

    pair_id = lax.rem(lane + 1, LANES) // 2
    per_group = LANES // 2 // LEVELS
    groups = channels // per_group
    sides[groups] = depth_here.astype(jnp.float32)

    def one_group(group, carry):
        packed = zero
        for slot in range(per_group):
            tracer = group * per_group + slot
            values = [field[tracer, k] for k in range(LEVELS)]
            for k in range(LEVELS):
                at = slot * LEVELS + k
                packed = jnp.where(pair_id == at, right(values[k], 2 * at), packed)
            diff = [(values[k + 1] - values[k]) * coef[6, k] for k in range(LEVELS - 1)]
            pair = [diff[0]] + [diff[k - 1] + diff[k] for k in range(1, LEVELS - 1)] + [diff[LEVELS - 2]]
            grad_x, grad_y = [], []
            for k in range(LEVELS):
                here, both = values[k], pair[k]
                grad_w = coef[0, k] * (here - right(here))
                grad_e = coef[1, k] * (right(here, -1) - here)
                grad_s = coef[2, k] * (here - pltpu.roll(here, 1, 0))
                flux_w = grad_w + coef[3, k] * (both + right(both))
                flux_e = grad_e + coef[4, k] * (both + right(both, -1))
                flux_s = grad_s + coef[5, k] * (both + pltpu.roll(both, 1, 0))
                grad_x.append(grad_w + grad_e)
                grad_y.append(grad_s + up_one(grad_s, 0))
                part[0, tracer, k] = here + (flux_e - flux_w) + (up_one(flux_s, 0) - flux_s)
            for k in range(LEVELS - 1):
                part[1, tracer, k] = grad_x[k] + grad_x[k + 1]
                part[2, tracer, k] = grad_y[k] + grad_y[k + 1]
                part[3, tracer, k] = diff[k]
        sides[group] = packed
        return carry

    lax.fori_loop(0, groups, one_group, 0)

    pl.semaphore_wait(barrier, jnp.where(bottom, 3, 4))

    def send(source, target, slot, device, send_slot=None):
        return pltpu.make_async_remote_copy(
            src_ref=source,
            dst_ref=target,
            send_sem=send_sem.at[slot if send_slot is None else send_slot],
            recv_sem=recv_sem.at[slot],
            device_id=device,
            device_id_type=MESH,
        )

    def to_north_halo(source, depth_row, device, first_send):
        copies = [send(depth_row, depth_north, 0, device, first_send)]
        for chunk in range(chunks):
            span = pl.ds(chunk * per_chunk, per_chunk)
            slot = 1 + chunk
            copies.append(send(source.at[span], from_north.at[span], slot, device, first_send + slot))
        return copies

    base = 1 + chunks
    own_south = depth.at[pl.ds(0, 1)]
    own_north = depth.at[pl.ds(ROWS - 1, 1)]
    fold = to_north_halo(row_north, own_north, north, base + 4)
    down = to_north_halo(row_south, own_south, south, 0)
    upward = [
        send(own_north, depth_south, base, north),
        send(row_north, from_south, base + 1, north),
    ]
    across = [
        send(sides, from_east, base + 2, west),
        send(sides, from_west, base + 3, east),
    ]

    @pl.when(top)
    def _():
        for copy in fold:
            copy.start()

    for copy in across:
        copy.start()

    @pl.when(jnp.logical_not(top))
    def _():
        for copy in upward:
            copy.start()

    @pl.when(jnp.logical_not(bottom))
    def _():
        for copy in down:
            copy.start()

    @pl.when(bottom)
    def _():
        from_south[...] = jnp.zeros_like(from_south)
        depth_south[...] = jnp.zeros_like(depth_south)

    for copy in across:
        copy.wait_recv()

    @pl.when(jnp.logical_not(bottom))
    def _():
        for copy in upward:
            copy.wait_recv()

    even = lax.rem(lane, 2) == 0
    at_edge = jnp.logical_or(lane == 0, lane == LANES - 1)
    side_level = lax.rem(pair_id, LEVELS)

    def beside(group):
        return jnp.where(even, right(from_west[group]), right(from_east[group], -1))

    def side_pair(values, mask):
        diff = (right(values, -2) - values) * mask
        return diff + right(diff, 2)

    west_limit = wide(from_west[groups][:, LANES - 1 : LANES]).astype(jnp.int32)
    east_limit = wide(from_east[groups][:, 0:1]).astype(jnp.int32)
    there_limit = jnp.where(even, west_limit, east_limit)
    here_limit = jnp.where(even, wide(depth_here[:, 0:1]), wide(depth_here[:, LANES - 1 : LANES]))
    there_mask, here_mask = below(there_limit, side_level + 1), below(here_limit, side_level + 1)
    side_mask = below(jnp.minimum(there_limit, here_limit), side_level)
    first_there, first_here = beside(0), sides[0]
    density_there = HALINE * right(first_there, -2 * LEVELS) - THERMAL * first_there
    density_here = HALINE * right(first_here, -2 * LEVELS) - THERMAL * first_here
    side_sign = jnp.where(even, -1.0, 1.0)
    side_slope = slope_of(
        side_sign * (density_there - density_here),
        side_mask,
        side_pair(density_there, there_mask) + side_pair(density_here, here_mask),
    )

    south_limit = wide(depth_south[...])
    south_mask = below(south_limit, row + 1)
    low_limit = wide(depth_here[0:1])
    low_mask = below(low_limit, row + 1)
    south_face = below(jnp.minimum(south_limit, low_limit), row)
    density_south = HALINE * from_south[1] - THERMAL * from_south[0]
    density_low = HALINE * row_south[1] - THERMAL * row_south[0]
    slope_south = slope_of(
        density_low - density_south,
        south_face,
        vertical_pair(density_south, south_mask, 0)[1] + vertical_pair(density_low, low_mask, 0)[1],
    )

    sum_x, sum_y = [], []
    for k in range(LEVELS):
        outer = jnp.where(at_edge, right(side_slope, -2 * k), 0.0)
        sum_x.append(coef[7, k] + outer)
        sum_y.append(coef[8, k] + jnp.where(row == 0, wide(slope_south[k : k + 1]), 0.0))
    lower_rows = jnp.where(row < ROWS - 1, 1.0, 0.0)
    side_cross = zero
    row_coef[2] = zero
    row_coef[3] = zero
    for k in range(LEVELS - 1):
        mean_x = 0.25 * (sum_x[k] + sum_x[k + 1])
        mean_y = 0.25 * (sum_y[k] + sum_y[k + 1])
        cross_x = CROSS * mean_x * coef[6, k]
        cross_y = CROSS * mean_y * coef[6, k]
        coef[0, k] = cross_x
        coef[1, k] = cross_y * lower_rows
        coef[2, k] = REDI_COEF * (mean_x * mean_x + mean_y * mean_y) * lower_rows
        row_coef[2, pl.ds(k, 1)] = cross_y[0:1]
        row_coef[3, pl.ds(k, 1)] = mean_x[ROWS - 1 : ROWS]
        ends = jnp.where(even, wide(cross_x[:, 0:1]), wide(cross_x[:, LANES - 1 : LANES]))
        side_cross = jnp.where(side_level == k, ends, side_cross)
    side_cross = side_cross * side_sign
    side_flux = jnp.where(pair_id < LEVELS, side_slope * side_sign * SLOPE_FLUX, 0.0)
    shift = 2 * LEVELS
    while shift < LANES:
        side_flux = side_flux + right(side_flux, shift)
        shift *= 2
    side_grad = REDI_COEF * side_mask

    for group in range(groups):
        own, other = sides[group], beside(group)
        grad = side_grad * (other - own)
        pair = side_pair(own, here_mask) + side_pair(other, there_mask)
        vertical = side_cross * (grad + right(grad, -2))
        edge[group] = vertical - right(vertical, 2) + grad + side_flux * pair

    def finish_group(group, carry):
        added = edge[group]
        for slot in range(per_group):
            tracer = group * per_group + slot
            above = None
            for k in range(LEVELS):
                at = slot * LEVELS + k
                total = part[0, tracer, k] + jnp.where(at_edge, right(added, -2 * at), 0.0)
                if k < LEVELS - 1:
                    vertical = (
                        coef[0, k] * part[1, tracer, k]
                        + coef[1, k] * part[2, tracer, k]
                        + coef[2, k] * part[3, tracer, k]
                    )
                    total = total + vertical
                if k > 0:
                    total = total - above
                above = vertical
                out[tracer, k] = total
        return carry

    lax.fori_loop(0, groups, finish_group, 0)

    grad_low, flux_low, cross_low = REDI_COEF * south_face, SLOPE_FLUX * slope_south, row_coef[2]

    def south_face_group(group, carry):
        for slot in range(per_group):
            tracer = group * per_group + slot
            own, other = row_south[tracer], from_south[tracer]
            grad = grad_low * (own - other)
            both = vertical_pair(own, low_mask, 0)[1] + vertical_pair(other, south_mask, 0)[1]
            vertical = cross_low * (grad + up_one(grad, 0))
            change = vertical - pltpu.roll(vertical, 1, 0) - (grad + flux_low * both)
            out[tracer, :, 0, :] = out[tracer, :, 0, :] + change
        return carry

    lax.fori_loop(0, groups, south_face_group, 0)

    source_lane = jnp.where(top, LANES - 1 - lane, lane)

    def arranged(values):
        return jnp.take_along_axis(values, source_lane, axis=1, mode="promise_in_bounds")

    high_limit = wide(depth_here[ROWS - 1 : ROWS])
    high_mask = below(high_limit, row + 1)
    density_high = HALINE * row_north[1] - THERMAL * row_north[0]
    strat_high = vertical_pair(density_high, high_mask, 0)[1]
    mean_x = row_coef[3]
    grad_in = REDI_COEF * row_coef[1]

    down[0].wait_recv()
    down[1].wait_recv()
    north_limit = arranged(wide(depth_north[...]))
    north_mask = below(north_limit, row + 1)
    north_face = below(jnp.minimum(high_limit, north_limit), row)
    density_north = arranged(HALINE * from_north[1] - THERMAL * from_north[0])
    strat_north = vertical_pair(density_north, north_mask, 0)[1]
    slope_north = slope_of(density_north - density_high, north_face, strat_high + strat_north)
    sum_n = slope_north + row_coef[0]
    mean_n = 0.25 * (sum_n + up_one(sum_n, 0))
    cross_n = CROSS * mean_n * high_mask
    square_n = REDI_COEF * (mean_x * mean_x + mean_n * mean_n)
    grad_n, flux_n = REDI_COEF * north_face, SLOPE_FLUX * slope_north

    def north_face_of(tracer):
        own, other = row_north[tracer], arranged(from_north[tracer])
        grad = grad_n * (other - own)
        diff, pair = vertical_pair(own, high_mask, 0)
        both = pair + vertical_pair(other, north_mask, 0)[1]
        grads = grad + grad_in * (own - row_inner[tracer])
        vertical = cross_n * (grads + up_one(grads, 0)) + square_n * diff
        change = vertical - pltpu.roll(vertical, 1, 0) + (grad + flux_n * both)
        out[tracer, :, ROWS - 1, :] = out[tracer, :, ROWS - 1, :] + change

    for chunk in range(chunks):
        if chunk:
            down[1 + chunk].wait_recv()
        for tracer in range(chunk * per_chunk, (chunk + 1) * per_chunk):
            north_face_of(tracer)

    for copy in across:
        copy.wait_send()

    @pl.when(top)
    def _():
        for copy in fold:
            copy.wait_send()

    @pl.when(jnp.logical_not(top))
    def _():
        for copy in upward:
            copy.wait_send()

    @pl.when(jnp.logical_not(bottom))
    def _():
        for copy in down:
            copy.wait_send()


def local(tracers, kmt):
    channels = tracers.shape[0]
    chunks = 4
    groups = channels * LEVELS * 2 // LANES
    row_array = VMEM((channels, LEVELS, LANES), jnp.float32)
    packed = VMEM((groups + 1, ROWS, LANES), jnp.float32)
    depth_row = VMEM((1, LANES), jnp.int32)
    anywhere = pl.BlockSpec(memory_space=pl.ANY)
    return pl.pallas_call(
        functools.partial(kernel, channels, chunks),
        out_shape=jax.ShapeDtypeStruct(tracers.shape, jnp.float32),
        in_specs=[anywhere, anywhere],
        out_specs=pl.BlockSpec(memory_space=VMEM),
        scratch_shapes=[
            VMEM(tracers.shape, jnp.float32),
            row_array, row_array, row_array, VMEM((ROWS, LANES), jnp.int32),
            row_array, row_array, depth_row, depth_row,
            packed, packed, packed,
            VMEM((9, LEVELS, ROWS, LANES), jnp.float32),
            VMEM((4,) + tracers.shape, jnp.float32),
            VMEM((groups, ROWS, LANES), jnp.float32),
            VMEM((4, LEVELS, LANES), jnp.float32),
            pltpu.SemaphoreType.DMA((5,)),
            pltpu.SemaphoreType.DMA((2 * chunks + 6,)),
            pltpu.SemaphoreType.DMA((chunks + 5,)),
        ],
        compiler_params=pltpu.CompilerParams(collective_id=0, has_side_effects=True),
        name="tracer_step",
    )(tracers, kmt)


def solution(mesh):
    return jax.shard_map(
        local,
        mesh=mesh,
        in_specs=(P(None, None, "lat", "lon"), P("lat", "lon")),
        out_specs=P(None, None, "lat", "lon"),
        check_vma=False,
    )
```

time: 48.8 us -> 29.7 us (0.61)
  Pallas kernels: 46.1 us -> 27 us
    pallas_call x1, Pallas kernels: 46.1 us -> 27 us  [local(): pl.pallas_call(functools.partial(kernel, channels, chunks), out_shape=jax...]
where the time goes in v2:
time: 29.7 us; the launch traced here: 29.6 us
  Pallas kernels  27 us (91%)
  local copies, waits for them, and re-layouts  2.52 us (8%)
    pallas_call x1, Pallas kernels, local(): pl.pallas_call(functools.partial(kernel, channels, chunks), out_shape=jax...  27 us
    unnamed x1, local copies, waits for them, and re-layouts  2.52 us

profile of v2, /device:TPU:27, one launch (start us, length us, event | category | flops | bytes accessed | tf_op | source)
XLA Modules:
  0.0 29.6 jit_solution(6309920417721999295)
XLA Ops:
  0.0 27.0 %tracer_step.1 = f32[40,8,8,128]{3,2,1,0:T(8,128)} custom-call(f32[40,8,8,128]{3,2,1,0:T(8,128)} %tracers.1, s32[8,128]{1,0:T(8,128)} %kmt.1), custom_call_target="tpu_custom_call" | custom-call | tf_op jit(solution)/shard_map/tracer_step/pallas_call | solution.py:409
  27.0 2.5 %copy.4 = f32[40,8,8,128]{3,2,1,0:T(8,128)} copy(f32[40,8,8,128]{3,2,1,0:T(8,128)} %tracer_step.1) | data formatting | bytes 2621440

commit v3 on v2

v3 whole, which is shorter than its diff:
```python
import functools

import jax
import jax.numpy as jnp
from jax import lax
from jax.experimental import pallas as pl
from jax.experimental.pallas import tpu as pltpu
from jax.sharding import PartitionSpec as P

THERMAL = 0.2
HALINE = 0.8
REDI_COEF = 0.1
SKEW_COEF = 0.05
SLOPE_MAX = 0.6
SLOPE_WIDTH = 0.2
SLOPE_FLUX = (REDI_COEF - SKEW_COEF) * 0.25
CROSS = (REDI_COEF + SKEW_COEF) * 0.25 / REDI_COEF

ROWS = 8
LANES = 128
LEVELS = 8
MESH = pl.DeviceIdType.MESH
VMEM = pltpu.VMEM


def taper(slope):
    return slope * 0.5 * (1.0 + jnp.tanh((SLOPE_MAX - jnp.abs(slope)) / SLOPE_WIDTH))


def slope_of(step, mask, strat_twice):
    return taper(step * mask / jnp.maximum(0.25 * strat_twice, 1.0))


def below(limit, level):
    return jnp.where(level < limit, 1.0, 0.0)


def vertical_pair(values, mask, axis):
    size = values.shape[axis]
    diff = (pltpu.roll(values, size - 1, axis) - values) * mask
    return diff, diff + pltpu.roll(diff, 1, axis)


def up_one(values, axis):
    return pltpu.roll(values, values.shape[axis] - 1, axis)


def kernel(
    channels, chunks, early, tracers, kmt, out,
    field, depth, from_south, from_north, depth_south, depth_north,
    sides, from_west, from_east,
    main, cross_x, coef, inner, edge, row_coef,
    load_sem, send_sem, recv_sem,
):
    lon, lat = lax.axis_index("lon"), lax.axis_index("lat")
    blocks, bands = lax.axis_size("lon"), lax.axis_size("lat")
    top, bottom = lat == bands - 1, lat == 0
    west = (lax.rem(lon + blocks - 1, blocks), lat)
    east = (lax.rem(lon + 1, blocks), lat)
    north = (jnp.where(top, blocks - 1 - lon, lon), jnp.where(top, lat, lat + 1))
    south = (lon, jnp.maximum(lat - 1, 0))
    per_chunk = channels // chunks
    per_group = LANES // 2 // LEVELS
    groups = channels // per_group

    barrier = pltpu.get_barrier_semaphore()
    for other in (north, west, east):
        pl.semaphore_signal(barrier, inc=1, device_id=other, device_id_type=MESH)

    @pl.when(jnp.logical_not(bottom))
    def _():
        pl.semaphore_signal(barrier, inc=1, device_id=south, device_id_type=MESH)

    loads = [
        pltpu.make_async_copy(kmt, depth, load_sem.at[0]),
        pltpu.make_async_copy(tracers, field, load_sem.at[1]),
    ]
    for load in loads:
        load.start()

    def send(source, target, slot, device, send_slot=None):
        return pltpu.make_async_remote_copy(
            src_ref=source,
            dst_ref=target,
            send_sem=send_sem.at[slot if send_slot is None else send_slot],
            recv_sem=recv_sem.at[slot],
            device_id=device,
            device_id_type=MESH,
        )

    def to_north_halo(own_row, device, first_send):
        copies = [send(kmt.at[pl.ds(own_row, 1)], depth_north, 0, device, first_send)]
        for chunk in range(chunks):
            span = pl.ds(chunk * per_chunk, per_chunk)
            slot = 1 + chunk
            source = tracers.at[span, :, own_row, :]
            copies.append(send(source, from_north.at[span], slot, device, first_send + slot))
        return copies

    base = 1 + chunks
    fold = to_north_halo(ROWS - 1, north, base + 4)
    down = to_north_halo(0, south, 0)
    upward = [
        send(kmt.at[pl.ds(ROWS - 1, 1)], depth_south, base, north),
        send(tracers.at[:, :, ROWS - 1, :], from_south, base + 1, north),
    ]
    across = [
        send(sides, from_east, base + 2, west),
        send(sides, from_west, base + 3, east),
    ]

    pl.semaphore_wait(barrier, jnp.where(bottom, 3, 4))

    @pl.when(jnp.logical_not(bottom))
    def _():
        for copy in down:
            copy.start()

    @pl.when(top)
    def _():
        for copy in fold[:early]:
            copy.start()

    @pl.when(jnp.logical_not(top))
    def _():
        for copy in upward:
            copy.start()

    for load in loads:
        load.wait()

    shape = (ROWS, LANES)
    lane = lax.broadcasted_iota(jnp.int32, shape, 1)
    row = lax.broadcasted_iota(jnp.int32, shape, 0)
    zero = jnp.zeros(shape, jnp.float32)
    depth_here = depth[...]

    def right(values, count=1):
        return pltpu.roll(values, count % LANES, 1)

    def wide(values):
        return jnp.broadcast_to(values, shape)

    pair_id = lax.rem(lane + 1, LANES) // 2
    sides[groups] = depth_here.astype(jnp.float32)
    for group in range(groups):
        packed = zero
        for at in range(LANES // 2):
            tracer, k = group * per_group + at // LEVELS, at % LEVELS
            packed = jnp.where(pair_id == at, right(field[tracer, k], 2 * at), packed)
        sides[group] = packed

    for copy in across:
        copy.start()

    @pl.when(top)
    def _():
        for copy in fold[early:]:
            copy.start()

    @pl.when(bottom)
    def _():
        from_south[...] = jnp.zeros_like(from_south)
        depth_south[...] = jnp.zeros_like(depth_south)

    density = [HALINE * field[1, k] - THERMAL * field[0, k] for k in range(LEVELS)]
    level_mask = [below(depth_here, k + 1) for k in range(LEVELS - 1)]
    strat_face = [(density[k + 1] - density[k]) * level_mask[k] for k in range(LEVELS - 1)]
    strat = [strat_face[0]]
    strat += [strat_face[k - 1] + strat_face[k] for k in range(1, LEVELS - 1)]
    strat += [strat_face[LEVELS - 2]]
    depth_left = jnp.minimum(depth_here, jnp.where(lane == 0, 0, right(depth_here)))
    depth_right = jnp.minimum(depth_here, jnp.where(lane == LANES - 1, 0, right(depth_here, -1)))
    depth_down = jnp.minimum(depth_here, jnp.where(row == 0, 0, pltpu.roll(depth_here, 1, 0)))
    at_edge = jnp.logical_or(lane == 0, lane == LANES - 1)
    inner_lanes = jnp.where(at_edge, 0.0, 1.0)
    inner_rows = jnp.where(jnp.logical_or(row == 0, row == ROWS - 1), 0.0, 1.0)
    sum_x, sum_y = [], []
    inner_slope = zero
    for k in range(LEVELS):
        mask_w, mask_e, mask_s = (below(limit, k) for limit in (depth_left, depth_right, depth_down))
        slope_w = slope_of(density[k] - right(density[k]), mask_w, strat[k] + right(strat[k]))
        slope_e = slope_of(right(density[k], -1) - density[k], mask_e, strat[k] + right(strat[k], -1))
        slope_s = slope_of(
            density[k] - pltpu.roll(density[k], 1, 0), mask_s, strat[k] + pltpu.roll(strat[k], 1, 0)
        )
        coef[0, k] = REDI_COEF * mask_w
        coef[1, k] = REDI_COEF * mask_e
        coef[2, k] = REDI_COEF * mask_s
        coef[3, k] = SLOPE_FLUX * slope_w
        coef[4, k] = SLOPE_FLUX * slope_e
        coef[5, k] = SLOPE_FLUX * slope_s
        coef[6, k] = level_mask[k] if k < LEVELS - 1 else zero
        sum_x.append(slope_w + slope_e)
        sum_y.append(slope_s + up_one(slope_s, 0))
        inner_slope = jnp.where(pair_id == k, right(sum_x[k], 2 * k), inner_slope)
        row_coef[0, pl.ds(k, 1)] = slope_s[1:2]
        row_coef[1, pl.ds(k, 1)] = REDI_COEF * mask_s[1:2]
        row_coef[2, pl.ds(k, 1)] = slope_s[ROWS - 1 : ROWS]
        row_coef[3, pl.ds(k, 1)] = REDI_COEF * mask_s[ROWS - 1 : ROWS]
    for k in range(LEVELS - 1):
        mean_x = 0.25 * (sum_x[k] + sum_x[k + 1]) * inner_lanes
        mean_y = 0.25 * (sum_y[k] + sum_y[k + 1]) * inner_rows
        coef[7, k] = CROSS * mean_x * level_mask[k]
        coef[8, k] = CROSS * mean_y * level_mask[k]
        coef[9, k] = REDI_COEF * (mean_x * mean_x + mean_y * mean_y)

    def one_group(group, carry):
        for slot in range(per_group):
            tracer = group * per_group + slot
            values = [field[tracer, k] for k in range(LEVELS)]
            diff = [(values[k + 1] - values[k]) * coef[6, k] for k in range(LEVELS - 1)]
            pair = [diff[0]] + [diff[k - 1] + diff[k] for k in range(1, LEVELS - 1)] + [diff[LEVELS - 2]]
            grad_x, grad_y, total = [], [], []
            for k in range(LEVELS):
                here, both = values[k], pair[k]
                grad_w = coef[0, k] * (here - right(here))
                grad_e = coef[1, k] * (right(here, -1) - here)
                grad_s = coef[2, k] * (here - pltpu.roll(here, 1, 0))
                flux_w = grad_w + coef[3, k] * (both + right(both))
                flux_e = grad_e + coef[4, k] * (both + right(both, -1))
                flux_s = grad_s + coef[5, k] * (both + pltpu.roll(both, 1, 0))
                grad_x.append(grad_w + grad_e)
                grad_y.append(grad_s + up_one(grad_s, 0))
                total.append(here + (flux_e - flux_w) + (up_one(flux_s, 0) - flux_s))
            above = None
            for k in range(LEVELS):
                added = total[k] if above is None else total[k] - above
                if k < LEVELS - 1:
                    both_x, both_y = grad_x[k] + grad_x[k + 1], grad_y[k] + grad_y[k + 1]
                    cross_x[tracer, k] = both_x
                    above = coef[7, k] * both_x + coef[8, k] * both_y + coef[9, k] * diff[k]
                    added = added + above
                main[tracer, k] = added
        return carry

    lax.fori_loop(0, groups, one_group, 0)

    for group in range(groups):
        packed = zero
        for at in range(LANES // 2):
            tracer, k = group * per_group + at // LEVELS, at % LEVELS
            if k < LEVELS - 1:
                packed = jnp.where(pair_id == at, right(cross_x[tracer, k], 2 * at), packed)
        inner[group] = packed

    source_lane = jnp.where(top, LANES - 1 - lane, lane)

    def mirrored(values):
        return jnp.take_along_axis(values, source_lane, axis=1, mode="promise_in_bounds")

    def row_terms(at, beyond, depth_beyond, arranged, first):
        sign = 1.0 if at else -1.0
        beside_row = at - 1 if at else 1
        limit = wide(depth_here[at : at + 1])
        mask = below(limit, row + 1)
        limit_beyond = arranged(wide(depth_beyond[...]))
        mask_beyond = below(limit_beyond, row + 1)
        face = below(jnp.minimum(limit, limit_beyond), row)
        density_row = HALINE * field[1, :, at, :] - THERMAL * field[0, :, at, :]
        density_beyond = arranged(HALINE * beyond[1] - THERMAL * beyond[0])
        slope = slope_of(
            sign * (density_beyond - density_row),
            face,
            vertical_pair(density_row, mask, 0)[1] + vertical_pair(density_beyond, mask_beyond, 0)[1],
        )
        sums = slope + row_coef[first]
        mean = 0.25 * (sums + up_one(sums, 0))
        cross, square = CROSS * mean * mask, REDI_COEF * mean * mean
        grad_face, flux_face, grad_in = REDI_COEF * face, sign * SLOPE_FLUX * slope, row_coef[first + 1]

        def add(tracer, result):
            own, other = field[tracer, :, at, :], arranged(beyond[tracer])
            step = grad_face * (other - own)
            diff, pair = vertical_pair(own, mask, 0)
            both = pair + vertical_pair(other, mask_beyond, 0)[1]
            grads = sign * (step + grad_in * (own - field[tracer, :, beside_row, :]))
            vertical = cross * (grads + up_one(grads, 0)) + square * diff
            change = vertical - pltpu.roll(vertical, 1, 0) + (step + flux_face * both)
            result[tracer, :, at, :] = result[tracer, :, at, :] + change

        return add

    @pl.when(jnp.logical_not(bottom))
    def _():
        for copy in upward:
            copy.wait_recv()

    add_south = row_terms(0, from_south, depth_south, lambda values: values, 0)
    for tracer in range(channels):
        add_south(tracer, main)

    def north_face(result):
        for copy in down[:2]:
            copy.wait_recv()
        add_north = row_terms(ROWS - 1, from_north, depth_north, mirrored, 2)
        for chunk in range(chunks):
            if chunk:
                down[1 + chunk].wait_recv()
            for tracer in range(chunk * per_chunk, (chunk + 1) * per_chunk):
                add_north(tracer, result)

    pl.when(jnp.logical_not(top))(functools.partial(north_face, main))

    even = lax.rem(lane, 2) == 0
    side_level = lax.rem(pair_id, LEVELS)
    side_sign = jnp.where(even, -1.0, 1.0)
    span = 2 * LEVELS

    def beside(group, shift=0):
        return jnp.where(even, right(from_west[group], 1 - shift), right(from_east[group], -1 - shift))

    def side_pair(values, mask):
        diff = (right(values, -2) - values) * mask
        return diff, diff + right(diff, 2)

    def every_tracer(values):
        values = jnp.where(pair_id < LEVELS, values, 0.0)
        total = values
        for shift in range(span, LANES, span):
            total = total + right(values, shift)
        return total

    here_limit = jnp.where(even, wide(depth_here[:, 0:1]), wide(depth_here[:, LANES - 1 : LANES]))
    here_mask = below(here_limit, side_level + 1)
    density_side = HALINE * right(sides[0], -span) - THERMAL * sides[0]
    strat_side = side_pair(density_side, here_mask)[1]

    for copy in across:
        copy.wait_recv()

    west_limit = wide(from_west[groups][:, LANES - 1 : LANES]).astype(jnp.int32)
    east_limit = wide(from_east[groups][:, 0:1]).astype(jnp.int32)
    there_limit = jnp.where(even, west_limit, east_limit)
    there_mask = below(there_limit, side_level + 1)
    side_mask = below(jnp.minimum(there_limit, here_limit), side_level)
    density_there = HALINE * beside(0, span) - THERMAL * beside(0)
    side_slope = slope_of(
        side_sign * (density_there - density_side),
        side_mask,
        strat_side + side_pair(density_there, there_mask)[1],
    )
    sums = side_slope + inner_slope
    mean = 0.25 * (sums + right(sums, -2))
    side_flux = every_tracer(SLOPE_FLUX * side_sign * side_slope)
    side_mean = every_tracer(mean)
    side_cross = CROSS * side_mean * here_mask
    side_square = REDI_COEF * side_mean * side_mean
    side_grad = REDI_COEF * side_mask
    for group in range(groups):
        own, other = sides[group], beside(group)
        step = side_grad * (other - own)
        diff, pair = side_pair(own, here_mask)
        grads = inner[group] + side_sign * (step + right(step, -2))
        vertical = side_cross * grads + side_square * diff
        change = vertical - right(vertical, 2) + step + side_flux * (pair + side_pair(other, there_mask)[1])
        edge[group] = change
    for group in range(groups):
        change = edge[group]
        for at in range(LANES // 2):
            tracer, k = group * per_group + at // LEVELS, at % LEVELS
            out[tracer, k] = main[tracer, k] + jnp.where(at_edge, right(change, -2 * at), 0.0)

    pl.when(top)(functools.partial(north_face, out))

    for copy in across:
        copy.wait_send()

    @pl.when(top)
    def _():
        for copy in fold:
            copy.wait_send()

    @pl.when(jnp.logical_not(top))
    def _():
        for copy in upward:
            copy.wait_send()

    @pl.when(jnp.logical_not(bottom))
    def _():
        for copy in down:
            copy.wait_send()


def local(tracers, kmt):
    channels = tracers.shape[0]
    chunks = 4
    early = 3
    groups = channels * LEVELS * 2 // LANES
    row_array = VMEM((channels, LEVELS, LANES), jnp.float32)
    packed = VMEM((groups + 1, ROWS, LANES), jnp.float32)
    depth_row = VMEM((1, LANES), jnp.int32)
    anywhere = pl.BlockSpec(memory_space=pl.ANY)
    return pl.pallas_call(
        functools.partial(kernel, channels, chunks, early),
        out_shape=VMEM(tracers.shape, jnp.float32),
        in_specs=[anywhere, anywhere],
        out_specs=pl.BlockSpec(memory_space=VMEM),
        scratch_shapes=[
            VMEM(tracers.shape, jnp.float32),
            VMEM((ROWS, LANES), jnp.int32),
            row_array, row_array, depth_row, depth_row,
            packed, packed, packed,
            VMEM(tracers.shape, jnp.float32),
            VMEM((channels, LEVELS - 1, ROWS, LANES), jnp.float32),
            VMEM((10, LEVELS, ROWS, LANES), jnp.float32),
            VMEM((groups, ROWS, LANES), jnp.float32),
            VMEM((groups, ROWS, LANES), jnp.float32),
            VMEM((4, LEVELS, LANES), jnp.float32),
            pltpu.SemaphoreType.DMA((2,)),
            pltpu.SemaphoreType.DMA((2 * chunks + 6,)),
            pltpu.SemaphoreType.DMA((chunks + 5,)),
        ],
        compiler_params=pltpu.CompilerParams(collective_id=0, has_side_effects=True),
        name="tracer_step",
    )(tracers, kmt)


def solution(mesh):
    return jax.shard_map(
        local,
        mesh=mesh,
        in_specs=(P(None, None, "lat", "lon"), P("lat", "lon")),
        out_specs=P(None, None, "lat", "lon"),
        check_vma=False,
    )
```

time: 29.7 us -> 22.9 us (0.77)
  Pallas kernels: 27 us -> 21.8 us
  local copies, waits for them, and re-layouts: 2.52 us -> 1.06 us
    pallas_call x1, Pallas kernels: 27 us -> 21.8 us  [local(): pl.pallas_call(functools.partial(kernel, channels, chunks, early), out_sh...]
    unnamed x1, local copies, waits for them, and re-layouts: 2.52 us -> 1.06 us
where the time goes in v3:
time: 22.9 us; the launch traced here: 22.8 us
  Pallas kernels  21.8 us (95%)
  local copies, waits for them, and re-layouts  1.06 us (5%)
    pallas_call x1, Pallas kernels, local(): pl.pallas_call(functools.partial(kernel, channels, chunks, early), out_sh...  21.8 us
    unnamed x1, local copies, waits for them, and re-layouts  1.06 us

profile of v3, /device:TPU:27, one launch (start us, length us, event | category | flops | bytes accessed | tf_op | source)
XLA Modules:
  0.0 22.8 jit_solution(17671274535062818016)
XLA Ops:
  0.0 21.8 %tracer_step.1 = f32[40,8,8,128]{3,2,1,0:T(8,128)S(1)} custom-call(f32[40,8,8,128]{3,2,1,0:T(8,128)} %tracers.1, s32[8,128]{1,0:T(8,128)} %kmt.1), custom_call_target="tpu_custom_call" | custom-call | tf_op jit(solution)/shard_map/tracer_step/pallas_call | solution.py:394
  21.8 1.1 %copy.4 = f32[40,8,8,128]{3,2,1,0:T(8,128)} copy(f32[40,8,8,128]{3,2,1,0:T(8,128)S(1)} %tracer_step.1) | data formatting | bytes 2621440

commit v4 on v3

v4 whole, which is shorter than its diff:
```python
import functools

import jax
import jax.numpy as jnp
from jax import lax
from jax.experimental import pallas as pl
from jax.experimental.pallas import tpu as pltpu
from jax.sharding import PartitionSpec as P

THERMAL = 0.2
HALINE = 0.8
REDI_COEF = 0.1
SKEW_COEF = 0.05
SLOPE_MAX = 0.6
SLOPE_WIDTH = 0.2
SLOPE_FLUX = (REDI_COEF - SKEW_COEF) * 0.25
CROSS = (REDI_COEF + SKEW_COEF) * 0.25 / REDI_COEF

ROWS = 8
LANES = 128
LEVELS = 8
SLAB = 16
MESH = pl.DeviceIdType.MESH
VMEM = pltpu.VMEM


def taper(slope):
    return slope * 0.5 * (1.0 + jnp.tanh((SLOPE_MAX - jnp.abs(slope)) / SLOPE_WIDTH))


def slope_of(step, mask, strat_twice):
    return taper(step * mask / jnp.maximum(0.25 * strat_twice, 1.0))


def below(limit, level):
    return jnp.where(level < limit, 1.0, 0.0)


def vertical_pair(values, mask, axis):
    size = values.shape[axis]
    diff = (pltpu.roll(values, size - 1, axis) - values) * mask
    return diff, diff + pltpu.roll(diff, 1, axis)


def tile(tracer, level):
    first = (tracer * LEVELS + level) * ROWS
    return pl.ds(first if isinstance(first, int) else pl.multiple_of(first, ROWS), ROWS)


def rows_of(tracer, row):
    return pl.ds(tracer * LEVELS * ROWS + row, LEVELS, stride=ROWS)


def up_one(values, axis):
    return pltpu.roll(values, values.shape[axis] - 1, axis)


def kernel(
    channels, chunks, early, tracers, flat, kmt, out,
    field, row_south, row_north, depth, from_south, from_north, depth_south, depth_north,
    sides, from_west, from_east,
    main, cross_x, coef, inner, edge, row_coef,
    load_sem, send_sem, recv_sem,
):
    lon, lat = lax.axis_index("lon"), lax.axis_index("lat")
    blocks, bands = lax.axis_size("lon"), lax.axis_size("lat")
    top, bottom = lat == bands - 1, lat == 0
    west = (lax.rem(lon + blocks - 1, blocks), lat)
    east = (lax.rem(lon + 1, blocks), lat)
    north = (jnp.where(top, blocks - 1 - lon, lon), jnp.where(top, lat, lat + 1))
    south = (lon, jnp.maximum(lat - 1, 0))
    patient = jnp.logical_or(lax.rem(lon, SLAB) == 0, jnp.logical_and(top, lax.rem(lon, SLAB) < SLAB // 2 - 1))
    per_chunk = channels // chunks
    per_group = LANES // 2 // LEVELS
    groups = channels // per_group

    barrier = pltpu.get_barrier_semaphore()
    for other in (north, west, east):
        pl.semaphore_signal(barrier, inc=1, device_id=other, device_id_type=MESH)

    @pl.when(jnp.logical_not(bottom))
    def _():
        pl.semaphore_signal(barrier, inc=1, device_id=south, device_id_type=MESH)

    rows_load = [
        pltpu.make_async_copy(tracers.at[:, :, ROWS - 1, :], row_north, load_sem.at[groups]),
        pltpu.make_async_copy(tracers.at[:, :, 0, :], row_south, load_sem.at[groups + 1]),
    ]
    depth_load = pltpu.make_async_copy(kmt, depth, load_sem.at[groups + 2])
    part = per_group * LEVELS * ROWS
    loads = [
        pltpu.make_async_copy(
            flat.at[pl.ds(group * part, part)], field.at[pl.ds(group * part, part)], load_sem.at[group]
        )
        for group in range(groups)
    ]
    depth_load.start()
    rows_load[0].start()
    for load in loads:
        load.start()
    rows_load[1].start()

    def send(source, target, slot, device, send_slot=None):
        return pltpu.make_async_remote_copy(
            src_ref=source,
            dst_ref=target,
            send_sem=send_sem.at[slot if send_slot is None else send_slot],
            recv_sem=recv_sem.at[slot],
            device_id=device,
            device_id_type=MESH,
        )

    def to_north_halo(own_row, values, device, first_send):
        copies = [send(depth.at[pl.ds(own_row, 1)], depth_north, 0, device, first_send)]
        for chunk in range(chunks):
            span = pl.ds(chunk * per_chunk, per_chunk)
            slot = 1 + chunk
            copies.append(send(values.at[span], from_north.at[span], slot, device, first_send + slot))
        return copies

    base = 1 + chunks
    fold = to_north_halo(ROWS - 1, row_north, north, base + 4)
    down = to_north_halo(0, row_south, south, 0)
    upward = [
        send(depth.at[pl.ds(ROWS - 1, 1)], depth_south, base, north),
        send(row_north, from_south, base + 1, north),
    ]
    across = [
        send(sides, from_east, base + 2, west),
        send(sides, from_west, base + 3, east),
    ]

    shape = (ROWS, LANES)
    lane = lax.broadcasted_iota(jnp.int32, shape, 1)
    row = lax.broadcasted_iota(jnp.int32, shape, 0)
    zero = jnp.zeros(shape, jnp.float32)

    def right(values, count=1):
        return pltpu.roll(values, count % LANES, 1)

    def wide(values):
        return jnp.broadcast_to(values, shape)

    pair_id = lax.rem(lane + 1, LANES) // 2
    at_edge = jnp.logical_or(lane == 0, lane == LANES - 1)

    def pack_columns():
        sides[groups] = depth[...].astype(jnp.float32)
        for group in range(groups):
            loads[group].wait()
            packed = zero
            for at in range(LANES // 2):
                tracer, k = group * per_group + at // LEVELS, at % LEVELS
                packed = jnp.where(pair_id == at, right(field[tile(tracer, k)], 2 * at), packed)
            sides[group] = packed

    def own_faces():
        depth_here = depth[...]
        density = [HALINE * field[tile(1, k)] - THERMAL * field[tile(0, k)] for k in range(LEVELS)]
        level_mask = [below(depth_here, k + 1) for k in range(LEVELS - 1)]
        strat_face = [(density[k + 1] - density[k]) * level_mask[k] for k in range(LEVELS - 1)]
        strat = [strat_face[0]]
        strat += [strat_face[k - 1] + strat_face[k] for k in range(1, LEVELS - 1)]
        strat += [strat_face[LEVELS - 2]]
        depth_left = jnp.minimum(depth_here, jnp.where(lane == 0, 0, right(depth_here)))
        depth_right = jnp.minimum(depth_here, jnp.where(lane == LANES - 1, 0, right(depth_here, -1)))
        depth_down = jnp.minimum(depth_here, jnp.where(row == 0, 0, pltpu.roll(depth_here, 1, 0)))
        inner_lanes = jnp.where(at_edge, 0.0, 1.0)
        inner_rows = jnp.where(jnp.logical_or(row == 0, row == ROWS - 1), 0.0, 1.0)
        sum_x, sum_y = [], []
        inner_slope = zero
        for k in range(LEVELS):
            mask_w, mask_e, mask_s = (below(limit, k) for limit in (depth_left, depth_right, depth_down))
            slope_w = slope_of(density[k] - right(density[k]), mask_w, strat[k] + right(strat[k]))
            slope_e = slope_of(right(density[k], -1) - density[k], mask_e, strat[k] + right(strat[k], -1))
            slope_s = slope_of(
                density[k] - pltpu.roll(density[k], 1, 0), mask_s, strat[k] + pltpu.roll(strat[k], 1, 0)
            )
            coef[0, k] = REDI_COEF * mask_w
            coef[1, k] = REDI_COEF * mask_e
            coef[2, k] = REDI_COEF * mask_s
            coef[3, k] = SLOPE_FLUX * slope_w
            coef[4, k] = SLOPE_FLUX * slope_e
            coef[5, k] = SLOPE_FLUX * slope_s
            coef[6, k] = level_mask[k] if k < LEVELS - 1 else zero
            sum_x.append(slope_w + slope_e)
            sum_y.append(slope_s + up_one(slope_s, 0))
            inner_slope = jnp.where(pair_id == k, right(sum_x[k], 2 * k), inner_slope)
            row_coef[0, pl.ds(k, 1)] = slope_s[1:2]
            row_coef[1, pl.ds(k, 1)] = REDI_COEF * mask_s[1:2]
            row_coef[2, pl.ds(k, 1)] = slope_s[ROWS - 1 : ROWS]
            row_coef[3, pl.ds(k, 1)] = REDI_COEF * mask_s[ROWS - 1 : ROWS]
        for k in range(LEVELS - 1):
            mean_x = 0.25 * (sum_x[k] + sum_x[k + 1]) * inner_lanes
            mean_y = 0.25 * (sum_y[k] + sum_y[k + 1]) * inner_rows
            coef[7, k] = CROSS * mean_x * level_mask[k]
            coef[8, k] = CROSS * mean_y * level_mask[k]
            coef[9, k] = REDI_COEF * (mean_x * mean_x + mean_y * mean_y)

        def one_group(group, carry):
            for slot in range(per_group):
                tracer = group * per_group + slot
                values = [field[tile(tracer, k)] for k in range(LEVELS)]
                diff = [(values[k + 1] - values[k]) * coef[6, k] for k in range(LEVELS - 1)]
                pair = [diff[0]] + [diff[k - 1] + diff[k] for k in range(1, LEVELS - 1)] + [diff[LEVELS - 2]]
                grad_x, grad_y, total = [], [], []
                for k in range(LEVELS):
                    here, both = values[k], pair[k]
                    grad_w = coef[0, k] * (here - right(here))
                    grad_e = coef[1, k] * (right(here, -1) - here)
                    grad_s = coef[2, k] * (here - pltpu.roll(here, 1, 0))
                    flux_w = grad_w + coef[3, k] * (both + right(both))
                    flux_e = grad_e + coef[4, k] * (both + right(both, -1))
                    flux_s = grad_s + coef[5, k] * (both + pltpu.roll(both, 1, 0))
                    grad_x.append(grad_w + grad_e)
                    grad_y.append(grad_s + up_one(grad_s, 0))
                    total.append(here + (flux_e - flux_w) + (up_one(flux_s, 0) - flux_s))
                above = None
                for k in range(LEVELS):
                    added = total[k] if above is None else total[k] - above
                    if k < LEVELS - 1:
                        both_x, both_y = grad_x[k] + grad_x[k + 1], grad_y[k] + grad_y[k + 1]
                        cross_x[tracer, k] = both_x
                        above = coef[7, k] * both_x + coef[8, k] * both_y + coef[9, k] * diff[k]
                        added = added + above
                    main[tile(tracer, k)] = added
            return carry

        coef[7, LEVELS - 1] = inner_slope
        lax.fori_loop(0, groups, one_group, 0)

        for group in range(groups):
            packed = zero
            for at in range(LANES // 2):
                tracer, k = group * per_group + at // LEVELS, at % LEVELS
                if k < LEVELS - 1:
                    packed = jnp.where(pair_id == at, right(cross_x[tracer, k], 2 * at), packed)
            inner[group] = packed

    def start_rows():
        for load in rows_load[1:]:
            load.wait()

        @pl.when(jnp.logical_not(bottom))
        def _():
            for copy in down:
                copy.start()

        @pl.when(jnp.logical_not(top))
        def _():
            for copy in upward:
                copy.start()

    def start_columns():
        for copy in across:
            copy.start()

    def start_fold(copies):
        for copy in copies:
            copy.start()

    slab_at = lax.rem(lon, SLAB)
    yielding = jnp.logical_and(top, jnp.logical_or(slab_at == SLAB - 4, slab_at == SLAB - 3))
    eager = jnp.logical_and(top, jnp.logical_not(jnp.logical_or(patient, yielding)))
    depth_load.wait()
    rows_load[0].wait()

    @pl.when(patient)
    def _():
        pack_columns()
        own_faces()

    pl.semaphore_wait(barrier, jnp.where(bottom, 3, 4))

    @pl.when(patient)
    def _():
        start_rows()
        start_columns()
        pl.when(top)(functools.partial(start_fold, fold))

    @pl.when(jnp.logical_not(patient))
    def _():
        pl.when(eager)(functools.partial(start_fold, fold[:early]))
        pack_columns()
        start_columns()
        start_rows()
        pl.when(eager)(functools.partial(start_fold, fold[early:]))
        own_faces()
        pl.when(yielding)(functools.partial(start_fold, fold))

    @pl.when(bottom)
    def _():
        from_south[...] = jnp.zeros_like(from_south)
        depth_south[...] = jnp.zeros_like(depth_south)

    depth_here = depth[...]
    inner_slope = coef[7, LEVELS - 1]

    source_lane = jnp.where(top, LANES - 1 - lane, lane)

    def mirrored(values):
        return jnp.take_along_axis(values, source_lane, axis=1, mode="promise_in_bounds")

    def row_terms(at, own_row, beyond, depth_beyond, arranged, first):
        sign = 1.0 if at else -1.0
        beside_row = at - 1 if at else 1
        limit = wide(depth_here[at : at + 1])
        mask = below(limit, row + 1)
        limit_beyond = arranged(wide(depth_beyond[...]))
        mask_beyond = below(limit_beyond, row + 1)
        face = below(jnp.minimum(limit, limit_beyond), row)
        density_row = HALINE * own_row[1] - THERMAL * own_row[0]
        density_beyond = arranged(HALINE * beyond[1] - THERMAL * beyond[0])
        slope = slope_of(
            sign * (density_beyond - density_row),
            face,
            vertical_pair(density_row, mask, 0)[1] + vertical_pair(density_beyond, mask_beyond, 0)[1],
        )
        sums = slope + row_coef[first]
        mean = 0.25 * (sums + up_one(sums, 0))
        cross, square = CROSS * mean * mask, REDI_COEF * mean * mean
        grad_face, flux_face, grad_in = REDI_COEF * face, sign * SLOPE_FLUX * slope, row_coef[first + 1]

        def add(tracer):
            own, other = own_row[tracer], arranged(beyond[tracer])
            step = grad_face * (other - own)
            diff, pair = vertical_pair(own, mask, 0)
            both = pair + vertical_pair(other, mask_beyond, 0)[1]
            grads = sign * (step + grad_in * (own - field[rows_of(tracer, beside_row)]))
            vertical = cross * (grads + up_one(grads, 0)) + square * diff
            change = vertical - pltpu.roll(vertical, 1, 0) + (step + flux_face * both)
            out[rows_of(tracer, at)] = out[rows_of(tracer, at)] + change

        return add

    even = lax.rem(lane, 2) == 0
    side_level = lax.rem(pair_id, LEVELS)
    side_sign = jnp.where(even, -1.0, 1.0)
    span = 2 * LEVELS

    def beside(group, shift=0):
        return jnp.where(even, right(from_west[group], 1 - shift), right(from_east[group], -1 - shift))

    def side_pair(values, mask):
        diff = (right(values, -2) - values) * mask
        return diff, diff + right(diff, 2)

    def every_tracer(values):
        values = jnp.where(pair_id < LEVELS, values, 0.0)
        total = values
        for shift in range(span, LANES, span):
            total = total + right(values, shift)
        return total

    here_limit = jnp.where(even, wide(depth_here[:, 0:1]), wide(depth_here[:, LANES - 1 : LANES]))
    here_mask = below(here_limit, side_level + 1)
    density_side = HALINE * right(sides[0], -span) - THERMAL * sides[0]
    strat_side = side_pair(density_side, here_mask)[1]

    for copy in across:
        copy.wait_recv()

    west_limit = wide(from_west[groups][:, LANES - 1 : LANES]).astype(jnp.int32)
    east_limit = wide(from_east[groups][:, 0:1]).astype(jnp.int32)
    there_limit = jnp.where(even, west_limit, east_limit)
    there_mask = below(there_limit, side_level + 1)
    side_mask = below(jnp.minimum(there_limit, here_limit), side_level)
    density_there = HALINE * beside(0, span) - THERMAL * beside(0)
    side_slope = slope_of(
        side_sign * (density_there - density_side),
        side_mask,
        strat_side + side_pair(density_there, there_mask)[1],
    )
    sums = side_slope + inner_slope
    mean = 0.25 * (sums + right(sums, -2))
    side_flux = every_tracer(SLOPE_FLUX * side_sign * side_slope)
    side_mean = every_tracer(mean)
    side_cross = CROSS * side_mean * here_mask
    side_square = REDI_COEF * side_mean * side_mean
    side_grad = REDI_COEF * side_mask
    for group in range(groups):
        own, other = sides[group], beside(group)
        step = side_grad * (other - own)
        diff, pair = side_pair(own, here_mask)
        grads = inner[group] + side_sign * (step + right(step, -2))
        vertical = side_cross * grads + side_square * diff
        change = vertical - right(vertical, 2) + step + side_flux * (pair + side_pair(other, there_mask)[1])
        edge[group] = change
    for group in range(groups):
        change = edge[group]
        for at in range(LANES // 2):
            tracer, k = group * per_group + at // LEVELS, at % LEVELS
            out[tile(tracer, k)] = main[tile(tracer, k)] + jnp.where(at_edge, right(change, -2 * at), 0.0)

    @pl.when(jnp.logical_not(bottom))
    def _():
        for copy in upward:
            copy.wait_recv()

    add_south = row_terms(0, row_south, from_south, depth_south, lambda values: values, 0)
    for tracer in range(channels):
        add_south(tracer)

    for copy in down[:2]:
        copy.wait_recv()
    add_north = row_terms(ROWS - 1, row_north, from_north, depth_north, mirrored, 2)
    for chunk in range(chunks):
        if chunk:
            down[1 + chunk].wait_recv()
        for tracer in range(chunk * per_chunk, (chunk + 1) * per_chunk):
            add_north(tracer)


    for copy in across:
        copy.wait_send()

    @pl.when(top)
    def _():
        for copy in fold:
            copy.wait_send()

    @pl.when(jnp.logical_not(top))
    def _():
        for copy in upward:
            copy.wait_send()

    @pl.when(jnp.logical_not(bottom))
    def _():
        for copy in down:
            copy.wait_send()


def local(tracers, kmt):
    channels = tracers.shape[0]
    chunks = 4
    early = 2
    groups = channels * LEVELS * 2 // LANES
    row_array = VMEM((channels, LEVELS, LANES), jnp.float32)
    packed = VMEM((groups + 1, ROWS, LANES), jnp.float32)
    depth_row = VMEM((1, LANES), jnp.int32)
    anywhere = pl.BlockSpec(memory_space=pl.ANY)
    flat = tracers.reshape(-1, LANES)
    updated = pl.pallas_call(
        functools.partial(kernel, channels, chunks, early),
        out_shape=VMEM(flat.shape, jnp.float32),
        in_specs=[anywhere, anywhere, anywhere],
        out_specs=pl.BlockSpec(memory_space=VMEM),
        scratch_shapes=[
            VMEM(flat.shape, jnp.float32),
            row_array, row_array, VMEM((ROWS, LANES), jnp.int32),
            row_array, row_array, depth_row, depth_row,
            packed, packed, packed,
            VMEM(flat.shape, jnp.float32),
            VMEM((channels, LEVELS - 1, ROWS, LANES), jnp.float32),
            VMEM((10, LEVELS, ROWS, LANES), jnp.float32),
            VMEM((groups, ROWS, LANES), jnp.float32),
            VMEM((groups, ROWS, LANES), jnp.float32),
            VMEM((4, LEVELS, LANES), jnp.float32),
            pltpu.SemaphoreType.DMA((groups + 3,)),
            pltpu.SemaphoreType.DMA((2 * chunks + 6,)),
            pltpu.SemaphoreType.DMA((chunks + 5,)),
        ],
        compiler_params=pltpu.CompilerParams(collective_id=0, has_side_effects=True),
        name="tracer_step",
    )(tracers, flat, kmt)
    return updated.reshape(tracers.shape)


def solution(mesh):
    return jax.shard_map(
        local,
        mesh=mesh,
        in_specs=(P(None, None, "lat", "lon"), P("lat", "lon")),
        out_specs=P(None, None, "lat", "lon"),
        check_vma=False,
    )
```

time: 22.9 us -> 21.7 us (0.948)
  the two profiles are of different devices: /device:TPU:27 before, /device:TPU:91 now
where the time goes in v4:
time: 21.7 us; the launch traced here: 21.5 us
  Pallas kernels  20.5 us (94%)
  local copies, waits for them, and re-layouts  1.06 us (5%)
    pallas_call x1, Pallas kernels, local(): pl.pallas_call(functools.partial(kernel, channels, chunks, early), out_sh...  20.5 us
    unnamed x1, local copies, waits for them, and re-layouts  1.06 us

profile of v4, /device:TPU:91, one launch (start us, length us, event | category | flops | bytes accessed | tf_op | source)
XLA Modules:
  0.0 21.5 jit_solution(8925856491253507455)
XLA Ops:
  0.0 20.5 %tracer_step.1 = f32[2560,128]{1,0:T(8,128)S(1)} custom-call(f32[40,8,8,128]{3,2,1,0:T(8,128)} %tracers.1, f32[2560,128]{1,0:T(8,128)} %bitcast.3, s32[8,128]{1,0:T(8,128)} %kmt.1), custom_call_target="tpu_custom_call" | custom-call | tf_op jit(solution)/shard_map/tracer_step/pallas_call | solution.py:443
  20.5 1.1 %copy.4 = f32[40,8,8,128]{3,2,1,0:T(8,128)} copy(f32[40,8,8,128]{3,2,1,0:T(8,128)S(1)} %bitcast.2) | data formatting | bytes 2621440

commit v5 on v4

--- a/solution.py
+++ b/solution.py
@@ -60,7 +60,7 @@
     field, row_south, row_north, depth, from_south, from_north, depth_south, depth_north,
     sides, from_west, from_east,
     main, cross_x, coef, inner, edge, row_coef,
-    load_sem, send_sem, recv_sem,
+    load_sem, send_sem, recv_sem, ready,
 ):
     lon, lat = lax.axis_index("lon"), lax.axis_index("lat")
     blocks, bands = lax.axis_size("lon"), lax.axis_size("lat")
@@ -74,9 +74,17 @@
     per_group = LANES // 2 // LEVELS
     groups = channels // per_group
 
+    slab_at = lax.rem(lon, SLAB)
+    opening = jnp.logical_and(slab_at == 0, jnp.logical_not(top))
+    closing = jnp.logical_and(slab_at == SLAB - 1, jnp.logical_not(top))
+
     barrier = pltpu.get_barrier_semaphore()
-    for other in (north, west, east):
+    for other in (north, west):
         pl.semaphore_signal(barrier, inc=1, device_id=other, device_id_type=MESH)
+
+    @pl.when(jnp.logical_not(closing))
+    def _():
+        pl.semaphore_signal(barrier, inc=1, device_id=east, device_id_type=MESH)
 
     @pl.when(jnp.logical_not(bottom))
     def _():
@@ -252,14 +260,13 @@
                 copy.start()
 
     def start_columns():
-        for copy in across:
-            copy.start()
+        across[1].start()
+        pl.when(jnp.logical_not(opening))(across[0].start)
 
     def start_fold(copies):
         for copy in copies:
             copy.start()
 
-    slab_at = lax.rem(lon, SLAB)
     yielding = jnp.logical_and(top, jnp.logical_or(slab_at == SLAB - 4, slab_at == SLAB - 3))
     eager = jnp.logical_and(top, jnp.logical_not(jnp.logical_or(patient, yielding)))
     depth_load.wait()
@@ -270,7 +277,11 @@
         pack_columns()
         own_faces()
 
-    pl.semaphore_wait(barrier, jnp.where(bottom, 3, 4))
+    pl.semaphore_wait(barrier, jnp.where(bottom, 3, 4) - jnp.where(opening, 1, 0))
+
+    @pl.when(closing)
+    def _():
+        pl.semaphore_signal(ready, inc=1, device_id=east, device_id_type=MESH)
 
     @pl.when(patient)
     def _():
@@ -283,10 +294,13 @@
         pl.when(eager)(functools.partial(start_fold, fold[:early]))
         pack_columns()
         start_columns()
+        pl.when(eager)(functools.partial(start_fold, fold[early:]))
         start_rows()
-        pl.when(eager)(functools.partial(start_fold, fold[early:]))
+        nearer = jnp.logical_and(yielding, slab_at == SLAB - 3)
+        pl.when(nearer)(functools.partial(start_fold, fold[:early]))
         own_faces()
-        pl.when(yielding)(functools.partial(start_fold, fold))
+        pl.when(jnp.logical_and(yielding, slab_at == SLAB - 4))(functools.partial(start_fold, fold[:early]))
+        pl.when(yielding)(functools.partial(start_fold, fold[early:]))
 
     @pl.when(bottom)
     def _():
@@ -321,7 +335,7 @@
         cross, square = CROSS * mean * mask, REDI_COEF * mean * mean
         grad_face, flux_face, grad_in = REDI_COEF * face, sign * SLOPE_FLUX * slope, row_coef[first + 1]
 
-        def add(tracer):
+        def add(tracer, result):
             own, other = own_row[tracer], arranged(beyond[tracer])
             step = grad_face * (other - own)
             diff, pair = vertical_pair(own, mask, 0)
@@ -329,9 +343,35 @@
             grads = sign * (step + grad_in * (own - field[rows_of(tracer, beside_row)]))
             vertical = cross * (grads + up_one(grads, 0)) + square * diff
             change = vertical - pltpu.roll(vertical, 1, 0) + (step + flux_face * both)
-            out[rows_of(tracer, at)] = out[rows_of(tracer, at)] + change
+            result[rows_of(tracer, at)] = result[rows_of(tracer, at)] + change
 
         return add
+
+    @pl.when(jnp.logical_not(bottom))
+    def _():
+        for copy in upward:
+            copy.wait_recv()
+
+    add_south = row_terms(0, row_south, from_south, depth_south, lambda values: values, 0)
+    for tracer in range(channels):
+        add_south(tracer, main)
+
+    def north_face(result):
+        for copy in down[:2]:
+            copy.wait_recv()
+        add_north = row_terms(ROWS - 1, row_north, from_north, depth_north, mirrored, 2)
+        for chunk in range(chunks):
+            if chunk:
+                down[1 + chunk].wait_recv()
+            for tracer in range(chunk * per_chunk, (chunk + 1) * per_chunk):
+                add_north(tracer, result)
+
+    pl.when(jnp.logical_not(top))(functools.partial(north_face, main))
+
+    @pl.when(opening)
+    def _():
+        pl.semaphore_wait(ready, 1)
+        across[0].start()
 
     even = lax.rem(lane, 2) == 0
     side_level = lax.rem(pair_id, LEVELS)
@@ -392,24 +432,7 @@
             tracer, k = group * per_group + at // LEVELS, at % LEVELS
             out[tile(tracer, k)] = main[tile(tracer, k)] + jnp.where(at_edge, right(change, -2 * at), 0.0)
 
-    @pl.when(jnp.logical_not(bottom))
-    def _():
-        for copy in upward:
-            copy.wait_recv()
-
-    add_south = row_terms(0, row_south, from_south, depth_south, lambda values: values, 0)
-    for tracer in range(channels):
-        add_south(tracer)
-
-    for copy in down[:2]:
-        copy.wait_recv()
-    add_north = row_terms(ROWS - 1, row_north, from_north, depth_north, mirrored, 2)
-    for chunk in range(chunks):
-        if chunk:
-            down[1 + chunk].wait_recv()
-        for tracer in range(chunk * per_chunk, (chunk + 1) * per_chunk):
-            add_north(tracer)
-
+    pl.when(top)(functools.partial(north_face, out))
 
     for copy in across:
         copy.wait_send()
@@ -459,6 +482,7 @@
             pltpu.SemaphoreType.DMA((groups + 3,)),
             pltpu.SemaphoreType.DMA((2 * chunks + 6,)),
             pltpu.SemaphoreType.DMA((chunks + 5,)),
+            pltpu.SemaphoreType.REGULAR,
         ],
         compiler_params=pltpu.CompilerParams(collective_id=0, has_side_effects=True),
         name="tracer_step",

time: 21.7 us -> 22.6 us (1.041)
  the two profiles are of different devices: /device:TPU:91 before, /device:TPU:27 now
where the time goes in v5:
time: 22.6 us; the launch traced here: 22.4 us
  Pallas kernels  21.4 us (95%)
  local copies, waits for them, and re-layouts  1.06 us (5%)
    pallas_call x1, Pallas kernels, local(): pl.pallas_call(functools.partial(kernel, channels, chunks, early), out_sh...  21.4 us
    unnamed x1, local copies, waits for them, and re-layouts  1.06 us

profile of v5, /device:TPU:27, one launch (start us, length us, event | category | flops | bytes accessed | tf_op | source)
XLA Modules:
  0.0 22.4 jit_solution(7345289282214410977)
XLA Ops:
  0.0 21.4 %tracer_step.1 = f32[2560,128]{1,0:T(8,128)S(1)} custom-call(f32[40,8,8,128]{3,2,1,0:T(8,128)} %tracers.1, f32[2560,128]{1,0:T(8,128)} %bitcast.3, s32[8,128]{1,0:T(8,128)} %kmt.1), custom_call_target="tpu_custom_call" | custom-call | tf_op jit(solution)/shard_map/tracer_step/pallas_call | solution.py:466
  21.4 1.1 %copy.4 = f32[40,8,8,128]{3,2,1,0:T(8,128)} copy(f32[40,8,8,128]{3,2,1,0:T(8,128)S(1)} %bitcast.2) | data formatting | bytes 2621440

commit v6 on v5

--- a/solution.py
+++ b/solution.py
@@ -294,13 +294,10 @@
         pl.when(eager)(functools.partial(start_fold, fold[:early]))
         pack_columns()
         start_columns()
+        start_rows()
         pl.when(eager)(functools.partial(start_fold, fold[early:]))
-        start_rows()
-        nearer = jnp.logical_and(yielding, slab_at == SLAB - 3)
-        pl.when(nearer)(functools.partial(start_fold, fold[:early]))
         own_faces()
-        pl.when(jnp.logical_and(yielding, slab_at == SLAB - 4))(functools.partial(start_fold, fold[:early]))
-        pl.when(yielding)(functools.partial(start_fold, fold[early:]))
+        pl.when(yielding)(functools.partial(start_fold, fold))
 
     @pl.when(bottom)
     def _():

time: 22.6 us -> 21.7 us (0.960)
  the two profiles are of different devices: /device:TPU:27 before, /device:TPU:91 now
where the time goes in v6:
time: 21.7 us; the launch traced here: 21.5 us
  Pallas kernels  20.5 us (94%)
  local copies, waits for them, and re-layouts  1.06 us (5%)
    pallas_call x1, Pallas kernels, local(): pl.pallas_call(functools.partial(kernel, channels, chunks, early), out_sh...  20.5 us
    unnamed x1, local copies, waits for them, and re-layouts  1.06 us

profile of v6, /device:TPU:91, one launch (start us, length us, event | category | flops | bytes accessed | tf_op | source)
XLA Modules:
  0.0 21.5 jit_solution(13078172888709044945)
XLA Ops:
  0.0 20.5 %tracer_step.1 = f32[2560,128]{1,0:T(8,128)S(1)} custom-call(f32[40,8,8,128]{3,2,1,0:T(8,128)} %tracers.1, f32[2560,128]{1,0:T(8,128)} %bitcast.3, s32[8,128]{1,0:T(8,128)} %kmt.1), custom_call_target="tpu_custom_call" | custom-call | tf_op jit(solution)/shard_map/tracer_step/pallas_call | solution.py:463
  20.5 1.1 %copy.4 = f32[40,8,8,128]{3,2,1,0:T(8,128)} copy(f32[40,8,8,128]{3,2,1,0:T(8,128)S(1)} %bitcast.2) | data formatting | bytes 2621440

commit v7 on v6

--- a/solution.py
+++ b/solution.py
@@ -237,6 +237,7 @@
         coef[7, LEVELS - 1] = inner_slope
         lax.fori_loop(0, groups, one_group, 0)
 
+    def pack_sums():
         for group in range(groups):
             packed = zero
             for at in range(LANES // 2):
@@ -276,6 +277,7 @@
     def _():
         pack_columns()
         own_faces()
+        pack_sums()
 
     pl.semaphore_wait(barrier, jnp.where(bottom, 3, 4) - jnp.where(opening, 1, 0))
 
@@ -298,6 +300,7 @@
         pl.when(eager)(functools.partial(start_fold, fold[early:]))
         own_faces()
         pl.when(yielding)(functools.partial(start_fold, fold))
+        pack_sums()
 
     @pl.when(bottom)
     def _():

time: 21.7 us -> 22.6 us (1.041)
  the two profiles are of different devices: /device:TPU:91 before, /device:TPU:27 now
where the time goes in v7:
time: 22.6 us; the launch traced here: 22.4 us
  Pallas kernels  21.4 us (95%)
  local copies, waits for them, and re-layouts  1.06 us (5%)
    pallas_call x1, Pallas kernels, local(): pl.pallas_call(functools.partial(kernel, channels, chunks, early), out_sh...  21.4 us
    unnamed x1, local copies, waits for them, and re-layouts  1.06 us

profile of v7, /device:TPU:27, one launch (start us, length us, event | category | flops | bytes accessed | tf_op | source)
XLA Modules:
  0.0 22.4 jit_solution(7839270788774167714)
XLA Ops:
  0.0 21.4 %tracer_step.1 = f32[2560,128]{1,0:T(8,128)S(1)} custom-call(f32[40,8,8,128]{3,2,1,0:T(8,128)} %tracers.1, f32[2560,128]{1,0:T(8,128)} %bitcast.3, s32[8,128]{1,0:T(8,128)} %kmt.1), custom_call_target="tpu_custom_call" | custom-call | tf_op jit(solution)/shard_map/tracer_step/pallas_call | solution.py:466
  21.4 1.1 %copy.4 = f32[40,8,8,128]{3,2,1,0:T(8,128)} copy(f32[40,8,8,128]{3,2,1,0:T(8,128)S(1)} %bitcast.2) | data formatting | bytes 2621440
